TPU v7x, 128 devices: a whole 4x4x4 slice. The times are simulated.
128 devices in a mesh: member: 8 (over x, core), region: 16 (over z, y).
Axes of the slice: x: 4, y: 4, z: 4, core: 2. Of those that a mesh axis runs over, the one named last changes fastest.
Arguments:
- ensemble: float32 [24, 32, 128, 512], P('member', 'region'), may hold values from -6 to 6
- obs_value: float32 [32, 128, 128], P(None, ('member', 'region')), may hold values from -6 to 6
- obs_error: float32 [32, 128, 128], P(None, ('member', 'region')), may hold values from 0.5 to 4
- obs_index: int32 [32, 128, 128], P(None, ('member', 'region')), may hold values from 0 to 511
- obs_count: int32 [32, 128], P(None, ('member', 'region')), may hold values from 1 to 128
Outputs:
- analysis: float32 [24, 32, 128, 512], P('member', 'region')
Inputs may be any that keep to these rules, and one draw needn't show every extreme that they name: `obs_index`: value v names field v // (256) (0 SST, 1 SSH) at cell v mod (256) of the block, cells row-major. `obs_count`: slots below a block's count are observations; the others are padding and carry no weight.
All inputs are finite; a program needn't handle non-finite values.
Results may differ from a plain program's by a relative error of at most 0.0001.
Values sent between devices are 32-bit elements; how exact they have to be, the bound alone decides.
A program may use at most 64 MiB of HBM per device.

v0:
```python
import math

import jax
import jax.numpy as jnp
from jax import lax
from jax.sharding import PartitionSpec as P

SIDE = 16
NS_ITERS = 6


LOC_SCALE = 12.0
INFLATION_FACTOR = 1.1


def cut_along(shard, dim, devices):
    shape = shard.shape
    blocks = shard.reshape(*shape[:dim], devices, shape[dim] // devices, *shape[dim + 1 :])
    return jnp.moveaxis(blocks, dim, 0)


def laid_out(blocks, dim):
    blocks = jnp.moveaxis(blocks, 0, dim)
    shape = blocks.shape
    return blocks.reshape(*shape[:dim], shape[dim] * shape[dim + 1], *shape[dim + 2 :])


def exchange_both(shard, axis, axes, splits, concats):
    sizes = [lax.axis_size(a) for a in axes]
    blocks = cut_along(shard, splits[0], sizes[0])
    blocks = jnp.moveaxis(cut_along(blocks, splits[1] + 1, sizes[1]), 0, 1)
    inside = blocks.shape[2:]
    blocks = blocks.reshape(-1, *inside)
    blocks = lax.all_to_all(blocks, axis, split_axis=0, concat_axis=0, tiled=True)
    blocks = laid_out(blocks.reshape(*sizes, *inside), concats[0] + 1)
    return laid_out(blocks, concats[1])


def padded_2(shard, sides, width):
    edges = {}
    for axis, dim in sides:
        devices, length = (lax.axis_size(axis), shard.shape[dim])
        up = [(i, (i + 1) % devices) for i in range(devices - 1)]
        last = lax.slice_in_dim(shard, length - width, length, axis=dim)
        first = lax.slice_in_dim(shard, 0, width, axis=dim)
        edges[dim] = (
            lax.ppermute(last, axis, up),
            lax.ppermute(first, axis, [(b, a) for a, b in up]),
        )
    done = []
    for _, dim in sides:
        low, high = edges[dim]
        around = [(width, width) if d in done else (0, 0) for d in range(shard.ndim)]
        shard = jnp.concatenate([jnp.pad(low, around), shard, jnp.pad(high, around)], axis=dim)
        done.append(dim)
    return shard


def batch_product(left, right):
    return jnp.einsum("...ij,...jk->...ik", left, right, precision=lax.Precision.HIGHEST)


def observe(ensemble, obs_value, obs_error, obs_index, obs_count):
    ens_mean = jnp.mean(ensemble, axis=0)
    anomaly = ensemble - ens_mean
    slot_index = lax.broadcasted_iota(jnp.int32, obs_index.shape, 2)
    live_slot = jnp.where(slot_index < obs_count[:, :, None], 1.0, 0.0).astype(jnp.float32)
    root_weight = jnp.sqrt(live_slot / obs_error)
    value_count = anomaly.shape[3]
    value_ids = lax.broadcasted_iota(jnp.int32, (1, 1, 1, value_count), 3)
    selector = jnp.where(obs_index[:, :, :, None] == value_ids, 1.0, 0.0).astype(jnp.float32)
    seen_anom = jnp.einsum("rcov,krcv->rcko", selector, anomaly, precision=lax.Precision.HIGHEST)
    seen_mean = jnp.einsum("rcov,rcv->rco", selector, ens_mean, precision=lax.Precision.HIGHEST)
    rescaled_values = root_weight[:, :, None] * seen_anom
    innovation = root_weight * (obs_value - seen_mean)
    cell_index = obs_index % (SIDE * SIDE)
    rowpos = (cell_index // SIDE).astype(jnp.float32)
    column_position = (cell_index % SIDE).astype(jnp.float32)
    stacked = jnp.concatenate(
        [rescaled_values, innovation[:, :, None], rowpos[:, :, None], column_position[:, :, None]],
        axis=2,
    )
    return (anomaly, ens_mean, stacked)


def analyze(anomaly, ens_mean, padded):
    ensemble_members = anomaly.shape[0]
    row_count = anomaly.shape[1]
    col_count = anomaly.shape[2]
    pieces = []
    for row_step in range(3):
        for col_step in range(3):
            pieces.append(padded[row_step : row_step + row_count, col_step : col_step + col_count])
    nearby = jnp.stack(pieces, axis=2)
    rescaled_values = nearby[:, :, :, :ensemble_members]
    innovation = nearby[:, :, :, ensemble_members]
    rowpos = nearby[:, :, :, ensemble_members + 1]
    column_position = nearby[:, :, :, ensemble_members + 2]
    offset_index = jnp.arange(9, dtype=jnp.int32)
    offset_row = (offset_index // 3 - 1).astype(jnp.float32) * SIDE
    offset_col = (offset_index % 3 - 1).astype(jnp.float32) * SIDE
    half_side = SIDE // 2
    point_index = jnp.arange(4, dtype=jnp.int32)
    center_row = (point_index // 2).astype(jnp.float32) * half_side + (half_side - 1) * 0.5
    center_col = (point_index % 2).astype(jnp.float32) * half_side + (half_side - 1) * 0.5
    row_gap = offset_row[:, None] + rowpos
    col_gap = offset_col[:, None] + column_position
    distance = (row_gap[:, :, None] - center_row[:, None, None]) ** 2 + (
        col_gap[:, :, None] - center_col[:, None, None]
    ) ** 2
    locality = jnp.exp(-distance / (2.0 * LOC_SCALE * LOC_SCALE))
    weighted = locality[:, :, :, :, None, :] * rescaled_values[:, :, None]
    gramian_total = jnp.einsum(
        "rcpnko,rcnjo->rcpkj", weighted, rescaled_values, precision=lax.Precision.HIGHEST
    )
    drive_vec = jnp.einsum(
        "rcpnko,rcno->rcpk", weighted, innovation, precision=lax.Precision.HIGHEST
    )
    identity_matrix = jnp.eye(ensemble_members, dtype=jnp.float32)
    precision_matrix = gramian_total + (ensemble_members - 1) / INFLATION_FACTOR * identity_matrix
    norm_scale = jnp.sqrt(jnp.sum(precision_matrix * precision_matrix, axis=(3, 4), keepdims=True))
    root_iter = precision_matrix / norm_scale
    inv_iter = jnp.broadcast_to(identity_matrix, precision_matrix.shape)
    for sweep_index in range(NS_ITERS):
        ns_step = 1.5 * identity_matrix - 0.5 * batch_product(inv_iter, root_iter)
        root_iter = batch_product(root_iter, ns_step)
        inv_iter = batch_product(ns_step, inv_iter)
    inv_root = inv_iter / jnp.sqrt(norm_scale)
    half_way = jnp.einsum("rcpkj,rcpj->rcpk", inv_root, drive_vec, precision=lax.Precision.HIGHEST)
    mean_w = jnp.einsum("rcpkj,rcpj->rcpk", inv_root, half_way, precision=lax.Precision.HIGHEST)
    weights = mean_w[..., :, None] + math.sqrt(ensemble_members - 1) * inv_root
    point_weights = weights.reshape(row_count, col_count, 2, 2, ensemble_members, ensemble_members)
    shaped = anomaly.reshape(ensemble_members, row_count, col_count, 2, 2, half_side, 2, half_side)
    updated = jnp.einsum(
        "jrcvaybx,rcabjk->krcvaybx", shaped, point_weights, precision=lax.Precision.HIGHEST
    )
    return ens_mean[None] + updated.reshape(anomaly.shape)


def local(ensemble, obs_value, obs_error, obs_index, obs_count):
    by_block = exchange_both(ensemble, ("member", "region"), ("member", "region"), (2, 2), (0, 1))
    anomaly, ens_mean, stacked = observe(by_block, obs_value, obs_error, obs_index, obs_count)
    with_halo = padded_2(stacked, ((("member", "region"), 1),), 1)
    padded = jnp.pad(with_halo, ((1, 1), (0, 0), (0, 0), (0, 0)))
    row_span = anomaly.shape[1] // 8

    def one_group(turn_index, result):
        first_row_index = turn_index * row_span
        part_anom = lax.dynamic_slice_in_dim(anomaly, first_row_index, row_span, 1)
        part_mean = lax.dynamic_slice_in_dim(ens_mean, first_row_index, row_span, 0)
        part_pad = lax.dynamic_slice_in_dim(padded, first_row_index, row_span + 2, 0)
        return lax.dynamic_update_slice_in_dim(
            result, analyze(part_anom, part_mean, part_pad), first_row_index, 1
        )

    result = lax.fori_loop(0, 8, one_group, jnp.zeros_like(anomaly))
    by_rows = lax.all_to_all(result, "region", split_axis=1, concat_axis=2, tiled=True)
    return lax.all_to_all(by_rows, "member", split_axis=0, concat_axis=2, tiled=True)


def solution(mesh):
    return jax.shard_map(
        local,
        mesh=mesh,
        in_specs=(
            P("member", "region", None, None),
            P(None, ("member", "region"), None),
            P(None, ("member", "region"), None),
            P(None, ("member", "region"), None),
            P(None, ("member", "region")),
        ),
        out_specs=P("member", "region", None, None),
        check_vma=False,
    )
```

profile of v0, /device:TPU:1, one launch (start us, length us, event | category | flops | bytes accessed | tf_op | source)
XLA Modules:
  0.0 295.5 jit_solution(3947123815600746661)
XLA Ops:
  0.0 3.8 %copy.142 = f32[3,2,8,16,512]{4,1,0,3,2:T(2,128)} copy(f32[3,2,8,16,512]{4,3,2,1,0:T(8,128)} %bitcast.309) | data formatting | bytes 3145728 | tf_op jit(solution)/shard_map/reshape | solution.py:18
  3.8 11.5 %all-to-all-start = ((f32[128,3,2,1,512]{4,2,1,3,0:T(2,128)}), f32[128,3,2,1,512]{4,2,1,3,0:T(2,128)S(1)}, u32[]{:S(2)}, u32[]{:S(2)}) async-start(f32[128,3,2,1,512]{4,2,1,3,0:T(2,128)} %bitcast.48), calls=%async_computation | async-start | bytes 3145728 | tf_op jit(solution)/shard_map/all_to_all | solution.py:34
  15.3 23.9 %all-to-all-done = f32[128,3,2,1,512]{4,2,1,3,0:T(2,128)S(1)} async-done(((f32[128,3,2,1,512]{4,2,1,3,0:T(2,128)}), f32[128,3,2,1,512]{4,2,1,3,0:T(2,128)S(1)}, u32[]{:S(2)}, u32[]{:S(2)}) %all-to-all-start) | async-done | bytes 1572896 | tf_op jit(solution)/shard_map/all_to_all | solution.py:34
  41.3 7.9 %fusion.55 = f32[32,1,128]{2,1,0:T(1,128)S(1)} fusion(f32[32,512,1]{1,2,0:T(1,128)S(1)} %reshape.530, s32[32,128]{1,0:T(8,128)S(1)} %bitcast.321), kind=kOutput, calls=%fused_computation.91 | convolution fusion | flops 29360128 | bytes 98304 | tf_op jit(solution)/shard_map/rcov,rcv->rco/dot_general | solution.py:73
  49.3 7.8 %fusion.69 = f32[32,1,24,128]{3,2,0,1:T(8,128)S(1)} fusion(f32[24,32,512]{2,0,1:T(8,128)S(1)} %bitcast_subtract_fusion, s32[32,128]{1,0:T(8,128)S(1)} %bitcast.322, f32[32,128]{1,0:T(8,128)S(1)} %get-tuple-element.210), kind=kOutput, calls=%fused_computation.112 | convolution fusion | flops 608272384 | bytes 1998848 | tf_op jit(solution)/shard_map/rcov,krcv->rcko/dot_general | solution.py:72
  57.2 2.9 collective-permute-start
  60.1 6.0 %collective-permute-start.1 = (f32[32,1,27,128]{3,2,0,1:T(8,128)S(1)}, f32[32,1,27,128]{3,2,0,1:T(8,128)}, u32[]{:S(2)}, u32[]{:S(2)}) collective-permute-start(f32[32,1,27,128]{3,2,0,1:T(8,128)S(1)} %pad_maximum_fusion), channel_id=1, source_target_pairs={{1,0},{2,1},{3,2},{4,3},{5,4},{6,5},{7,6},{8,7},{9,8},{10,9},{11,1... | collective-permute-start | bytes 1327112 | tf_op jit(solution)/shard_map/ppermute | solution.py:48
  66.2 1.3 broadcast_subtract_fusion
  67.5 3.5 %collective-permute-done = f32[32,1,27,128]{3,2,0,1:T(8,128)S(1)} collective-permute-done((f32[32,1,27,128]{3,2,0,1:T(8,128)S(1)}, f32[32,1,27,128]{3,2,0,1:T(8,128)S(1)}, u32[]{:S(2)}, u32[]{:S(2)}) %collective-permute-start) | collective-permute-done | bytes 442400 | tf_op jit(solution)/shard_map/ppermute | solution.py:47
  71.1 6.8 %collective-permute-done.1 = f32[32,1,27,128]{3,2,0,1:T(8,128)} collective-permute-done((f32[32,1,27,128]{3,2,0,1:T(8,128)S(1)}, f32[32,1,27,128]{3,2,0,1:T(8,128)}, u32[]{:S(2)}, u32[]{:S(2)}) %collective-permute-start.1) | collective-permute-done | bytes 442400 | tf_op jit(solution)/shard_map/ppermute | solution.py:48
  77.9 1.2 select_maximum_fusion
  79.1 1.3 broadcast_in_dim.83.clone
  80.4 159.7 %while.16 = (s32[]{:T(128)}, f32[24,32,1,512]{3,0,2,1:T(8,128)}, f32[32,1,512]{2,0,1:T(8,128)S(1)}, f32[34,3,27,128]{3,2,0,1:T(8,128)S(1)}, f32[24,32,1,512]{3,0...) while((s32[]{:T(128)}, f32[24,32,1,512]{3,0,2,1:T(8,128)}, ...), condition=%wide.region_3.4_spmd, body=%wide.region_1.3_spmd.sunk | while | flops 193469024 | bytes 8862404 | solution.py:156
  81.1 4.9 %fusion.273 = f32[4,4,24,1]{2,3,1,0:T(1,128)S(1)} fusion(f32[4,9,24,128]{3,2,1,0:T(8,128)S(1)} %slice_bitcast_fusion.2, f32[4,4,9,128]{3,2,1,0:T(8,128)S(1)} %multiply_exponential_fusion.2, f32[4,9,128,1,1]{2,0,1,3,4:T(4,128)S(1)} %bitcast.311), kind=kOutput, calls=%fused_computation.21.clone.1 | convolution fusion | flops 5750784 | bytes 536064 | tf_op jit(solution)/shard_map/while/body/eval_jaxpr/rcpnko,rcno->rcpk/dot_general | solution.py:116
  86.0 1.8 multiply_reduce_fusion.2
  101.0 4.9 %fusion.273 = f32[4,4,24,1]{2,3,1,0:T(1,128)S(1)} fusion(f32[4,9,24,128]{3,2,1,0:T(8,128)S(1)} %slice_bitcast_fusion.2, f32[4,4,9,128]{3,2,1,0:T(8,128)S(1)} %multiply_exponential_fusion.2, f32[4,9,128,1,1]{2,0,1,3,4:T(4,128)S(1)} %bitcast.311), kind=kOutput, calls=%fused_computation.21.clone.1 | convolution fusion | flops 5750784 | bytes 536064 | tf_op jit(solution)/shard_map/while/body/eval_jaxpr/rcpnko,rcno->rcpk/dot_general | solution.py:116
  106.0 1.8 multiply_reduce_fusion.2
  121.0 4.9 %fusion.273 = f32[4,4,24,1]{2,3,1,0:T(1,128)S(1)} fusion(f32[4,9,24,128]{3,2,1,0:T(8,128)S(1)} %slice_bitcast_fusion.2, f32[4,4,9,128]{3,2,1,0:T(8,128)S(1)} %multiply_exponential_fusion.2, f32[4,9,128,1,1]{2,0,1,3,4:T(4,128)S(1)} %bitcast.311), kind=kOutput, calls=%fused_computation.21.clone.1 | convolution fusion | flops 5750784 | bytes 536064 | tf_op jit(solution)/shard_map/while/body/eval_jaxpr/rcpnko,rcno->rcpk/dot_general | solution.py:116
  125.9 1.8 multiply_reduce_fusion.2
  141.0 4.9 %fusion.273 = f32[4,4,24,1]{2,3,1,0:T(1,128)S(1)} fusion(f32[4,9,24,128]{3,2,1,0:T(8,128)S(1)} %slice_bitcast_fusion.2, f32[4,4,9,128]{3,2,1,0:T(8,128)S(1)} %multiply_exponential_fusion.2, f32[4,9,128,1,1]{2,0,1,3,4:T(4,128)S(1)} %bitcast.311), kind=kOutput, calls=%fused_computation.21.clone.1 | convolution fusion | flops 5750784 | bytes 536064 | tf_op jit(solution)/shard_map/while/body/eval_jaxpr/rcpnko,rcno->rcpk/dot_general | solution.py:116
  145.9 1.8 multiply_reduce_fusion.2
  160.9 4.9 %fusion.273 = f32[4,4,24,1]{2,3,1,0:T(1,128)S(1)} fusion(f32[4,9,24,128]{3,2,1,0:T(8,128)S(1)} %slice_bitcast_fusion.2, f32[4,4,9,128]{3,2,1,0:T(8,128)S(1)} %multiply_exponential_fusion.2, f32[4,9,128,1,1]{2,0,1,3,4:T(4,128)S(1)} %bitcast.311), kind=kOutput, calls=%fused_computation.21.clone.1 | convolution fusion | flops 5750784 | bytes 536064 | tf_op jit(solution)/shard_map/while/body/eval_jaxpr/rcpnko,rcno->rcpk/dot_general | solution.py:116
  165.9 1.8 multiply_reduce_fusion.2
  180.9 4.9 %fusion.273 = f32[4,4,24,1]{2,3,1,0:T(1,128)S(1)} fusion(f32[4,9,24,128]{3,2,1,0:T(8,128)S(1)} %slice_bitcast_fusion.2, f32[4,4,9,128]{3,2,1,0:T(8,128)S(1)} %multiply_exponential_fusion.2, f32[4,9,128,1,1]{2,0,1,3,4:T(4,128)S(1)} %bitcast.311), kind=kOutput, calls=%fused_computation.21.clone.1 | convolution fusion | flops 5750784 | bytes 536064 | tf_op jit(solution)/shard_map/while/body/eval_jaxpr/rcpnko,rcno->rcpk/dot_general | solution.py:116
  185.8 1.8 multiply_reduce_fusion.2
  200.9 4.9 %fusion.273 = f32[4,4,24,1]{2,3,1,0:T(1,128)S(1)} fusion(f32[4,9,24,128]{3,2,1,0:T(8,128)S(1)} %slice_bitcast_fusion.2, f32[4,4,9,128]{3,2,1,0:T(8,128)S(1)} %multiply_exponential_fusion.2, f32[4,9,128,1,1]{2,0,1,3,4:T(4,128)S(1)} %bitcast.311), kind=kOutput, calls=%fused_computation.21.clone.1 | convolution fusion | flops 5750784 | bytes 536064 | tf_op jit(solution)/shard_map/while/body/eval_jaxpr/rcpnko,rcno->rcpk/dot_general | solution.py:116
  205.8 1.8 multiply_reduce_fusion.2
  220.8 4.9 %fusion.273 = f32[4,4,24,1]{2,3,1,0:T(1,128)S(1)} fusion(f32[4,9,24,128]{3,2,1,0:T(8,128)S(1)} %slice_bitcast_fusion.2, f32[4,4,9,128]{3,2,1,0:T(8,128)S(1)} %multiply_exponential_fusion.2, f32[4,9,128,1,1]{2,0,1,3,4:T(4,128)S(1)} %bitcast.311), kind=kOutput, calls=%fused_computation.21.clone.1 | convolution fusion | flops 5750784 | bytes 536064 | tf_op jit(solution)/shard_map/while/body/eval_jaxpr/rcpnko,rcno->rcpk/dot_general | solution.py:116
  225.8 1.8 multiply_reduce_fusion.2
  240.2 23.2 %all_to_all.41 = f32[24,32,1,512]{3,0,2,1:T(8,128)S(1)} all-to-all(f32[24,32,1,512]{3,0,2,1:T(8,128)} %get-tuple-element.173), channel_id=1, replica_groups=mesh['member'=8,'region'=16] {'region'}, dimensions={1} | all-to-all | bytes 3145728 | tf_op jit(solution)/shard_map/all_to_all | solution.py:157
  264.6 29.3 %all_to_all.42 = f32[24,2,16,512]{3,1,2,0:T(2,128)S(1)} all-to-all(f32[24,2,16,512]{3,1,2,0:T(2,128)S(1)} %copy.157), channel_id=1, replica_groups=mesh['member'=8,'region'=16] {'member'}, dimensions={0} | all-to-all | bytes 3145728 | tf_op jit(solution)/shard_map/all_to_all | solution.py:158
  294.2 1.4 copy.159
  (431 shorter events, 107.1 us)
Async XLA Ops:
  3.8 11.5 %copy-start.2 = (s32[32,1,128]{2,1,0:T(1,128)S(1)}, s32[32,1,128]{2,1,0:T(1,128)}, u32[]{:S(2)}) copy-start(s32[32,1,128]{2,1,0:T(1,128)} %param.10) | copy-start | bytes 49156
  3.8 35.5 %all-to-all-start = ((f32[128,3,2,1,512]{4,2,1,3,0:T(2,128)}), f32[128,3,2,1,512]{4,2,1,3,0:T(2,128)S(1)}, u32[]{:S(2)}, u32[]{:S(2)}) async-start(f32[128,3,2,1,512]{4,2,1,3,0:T(2,128)} %bitcast.48), calls=%async_computation | async-start | bytes 3145728 | tf_op jit(solution)/shard_map/all_to_all | solution.py:34
  41.2 8.0 %copy-start = (f32[32,1,128]{2,1,0:T(1,128)S(1)}, f32[32,1,128]{2,1,0:T(1,128)}, u32[]{:S(2)}) copy-start(f32[32,1,128]{2,1,0:T(1,128)} %param.9) | copy-start | bytes 49156
  41.2 8.0 %copy-start.1 = (f32[32,1,128]{2,1,0:T(1,128)S(1)}, f32[32,1,128]{2,1,0:T(1,128)}, u32[]{:S(2)}) copy-start(f32[32,1,128]{2,1,0:T(1,128)} %param.8) | copy-start | bytes 49156
  41.2 8.0 %copy-start.3 = (s32[32,1]{0,1:T(1,128)S(1)}, s32[32,1]{0,1:T(1,128)}, u32[]{:S(2)}) copy-start(s32[32,1]{0,1:T(1,128)} %param.11) | copy-start | bytes 388
  57.2 13.8 %collective-permute-start = (f32[32,1,27,128]{3,2,0,1:T(8,128)S(1)}, f32[32,1,27,128]{3,2,0,1:T(8,128)S(1)}, u32[]{:S(2)}, u32[]{:S(2)}) collective-permute-start(f32[32,1,27,128]{3,2,0,1:T(8,128)S(1)} %pad_maximum_fusion), channel_id=1, source_target_pairs={{0,1},{1,2},{2,3},{3,4},{4,5},{5,6},{6,7},{7,8},{8,9},{9,10},{10,1... | collective-permute-start | bytes 1327112 | tf_op jit(solution)/shard_map/ppermute | solution.py:47
  60.1 17.7 %collective-permute-start.1 = (f32[32,1,27,128]{3,2,0,1:T(8,128)S(1)}, f32[32,1,27,128]{3,2,0,1:T(8,128)}, u32[]{:S(2)}, u32[]{:S(2)}) collective-permute-start(f32[32,1,27,128]{3,2,0,1:T(8,128)S(1)} %pad_maximum_fusion), channel_id=1, source_target_pairs={{1,0},{2,1},{3,2},{4,3},{5,4},{6,5},{7,6},{8,7},{9,8},{10,9},{11,1... | collective-permute-start | bytes 1327112 | tf_op jit(solution)/shard_map/ppermute | solution.py:48
where the time goes:
time: 296 us
  matrix products  146 us (49%)
  blocking collectives  52.4 us (18%)
  waiting for transfers between devices  34.2 us (12%)
  local copies, waits for them, and re-layouts  30.4 us (10%)
  starting transfers between devices  20.4 us (7%)
  other arithmetic  9.16 us (3%)
    dot_general x136, matrix products, batch_product(): jnp.einsum('...ij,...jk->...ik', left, right, precision=lax.Precision.HIG...  62 us
    dot_general x8, matrix products, analyze(): jnp.einsum('rcpnko,rcno->rcpk', weighted, innovation, precision=lax.Preci...  39.3 us
    all_to_all x1, blocking collectives, local(): lax.all_to_all(by_rows, 'member', split_axis=0, concat_axis=2, tiled=True)  29.3 us
    all_to_all x1, waiting for transfers between devices, exchange_both(): lax.all_to_all(blocks, axis, split_axis=0, concat_axis=0, tiled=True)  23.9 us
    all_to_all x1, blocking collectives, local(): lax.all_to_all(result, 'region', split_axis=1, concat_axis=2, tiled=True)  23.2 us
    dot_general x8, matrix products, analyze(): jnp.einsum('rcpnko,rcnjo->rcpkj', weighted, rescaled_values, precision=la...  14.5 us
    all_to_all x1, starting transfers between devices, exchange_both(): lax.all_to_all(blocks, axis, split_axis=0, concat_axis=0, tiled=True)  11.5 us
    dynamic_slice x16, local copies, waits for them, and re-layouts, one_group(): part_anom = lax.dynamic_slice_in_dim(anomaly, first_row_index, row_span, 1)  10.2 us
  transfers between devices with their start and end apart: 3, of which 3 were waited for; matrix products, arithmetic and copies ran while one was open for 0% of the time, Pallas kernels for 0%

commit v1 on v0

v1 whole, which is shorter than its diff:
```python
import functools
import math

import jax
import jax.numpy as jnp
from jax import lax
from jax.experimental import pallas as pl
from jax.experimental.pallas import tpu as pltpu
from jax.sharding import PartitionSpec as P

MESH = pl.DeviceIdType.MESH
F32 = jnp.float32
BF16 = jnp.bfloat16

SIDE = 16
OBS = 128
NS_ITERS = 6
VALS = 512
K = 24
BROWS = 32
BCOLS = 128
LOC_SCALE = 12.0
INFLATION_FACTOR = 1.1
NM = 8
NR = 16
MINE = K // NM
ROWS = BROWS // NR
COLS = BCOLS // NM
GROUP = 8
CHUNKS = [(g, i) for g in range(COLS // GROUP) for i in range(ROWS)]
STACK = 32
PAIRS = 52 * 8


def pair_row(k, group):
    first = k // 8
    return (0, 192, 320)[first] + (k % 8) * 8 * (3 - first) + 8 * (group - first)


DRIVE = 384


def dev(m, r):
    return (lax.rem(m + NM, NM), lax.rem(r + NR, NR))


def remote(src, dst, send, recv, device):
    return pltpu.make_async_remote_copy(
        src_ref=src, dst_ref=dst, send_sem=send, recv_sem=recv, device_id=device, device_id_type=MESH
    )


def tri_product(dst, a, b, post):
    for ga in range(3):
        groups = list(range(ga, 3))

        def rows4(t, carry, ga=ga, groups=groups):
            base = (ga * 8 + t * 4) * K
            acc = [[None] * len(groups) for _ in range(4)]
            for k in range(K):
                bv = [b[pl.ds(k * K + 8 * gj, 8), :] for gj in groups]
                for u in range(4):
                    av = jnp.broadcast_to(a[pl.ds(base + u * K + k, 1), :], (8, 128))
                    for n in range(len(groups)):
                        term = av * bv[n]
                        acc[u][n] = term if acc[u][n] is None else acc[u][n] + term
            for u in range(4):
                for n, gj in enumerate(groups):
                    dst[pl.ds(base + u * K + 8 * gj, 8), :] = post(acc[u][n], ga * 8 + t * 4 + u, gj)
            return carry

        lax.fori_loop(0, 2, rows4, 0)
    fill_lower(dst)


def fill_lower(dst):
    for i in range(8, K):
        for gj in range(i // 8):
            dst[pl.ds(i * K + 8 * gj, 8), :] = dst[pl.ds(8 * gj * K + i, 8, stride=K), :]


def unit(i, gj):
    return jnp.where(lax.broadcasted_iota(jnp.int32, (8, 128), 0) + 8 * gj == i, 1.0, 0.0).astype(F32)


def newton_schulz(gram, wts, y, z, mm, tmp):
    for k in range(K):
        for gj in range(k // 8, 3):
            y[pl.ds(k * K + 8 * gj, 8), :] = gram[pl.ds(pair_row(k, gj), 8), :] + (K - 1) / INFLATION_FACTOR * unit(k, gj)
    fill_lower(y)
    square = jnp.zeros((8, 128), F32)
    for t in range(K * 3):
        v = y[pl.ds(8 * t, 8), :]
        square = square + v * v
    norm = jnp.sqrt(jnp.sum(square, axis=0, keepdims=True))
    inv_norm = 1.0 / norm
    for k in range(K):
        for gj in range(3):
            rows = pl.ds(k * K + 8 * gj, 8)
            v = y[rows, :] * inv_norm
            y[rows, :] = v
            m = 1.5 * unit(k, gj) - 0.5 * v
            mm[rows, :] = m
            z[rows, :] = m
    same = lambda v, i, gj: v
    step_of = lambda v, i, gj: 1.5 * unit(i, gj) - 0.5 * v
    tri_product(tmp, y, mm, same)

    def copy(dst, src):
        for t in range(K * 3):
            dst[pl.ds(8 * t, 8), :] = src[pl.ds(8 * t, 8), :]

    copy(y, tmp)

    def sweep(_, carry):
        tri_product(mm, z, y, step_of)
        tri_product(tmp, y, mm, same)
        copy(y, tmp)
        tri_product(tmp, mm, z, same)
        copy(z, tmp)
        return carry

    lax.fori_loop(0, NS_ITERS - 2, sweep, 0)
    tri_product(mm, z, y, step_of)
    tri_product(tmp, mm, z, same)
    scale = 1.0 / jnp.sqrt(norm)

    def apply(vector):
        acc = [jnp.zeros((8, 128), F32) for _ in range(3)]
        for k in range(K):
            row = vector[k // 8][k % 8 : k % 8 + 1, :]
            for gj in range(3):
                acc[gj] = acc[gj] + tmp[pl.ds(k * K + 8 * gj, 8), :] * row
        return [v * scale for v in acc]

    drive = [gram[pl.ds(DRIVE + 8 * gj, 8), :] for gj in range(3)]
    mean_w = apply(apply(drive))
    root = scale * math.sqrt(K - 1)
    for j in range(K):
        row = mean_w[j // 8][j % 8 : j % 8 + 1, :]
        for gj in range(3):
            rows = pl.ds(j * K + 8 * gj, 8)
            wts[rows, :] = tmp[rows, :] * root + row


def gather_chunk(x, obs, stack, means, g, i):
    cols = pl.ds(g * GROUP, GROUP)
    total = x[0, i, cols, :]
    for k in range(1, K):
        total = total + x[k, i, cols, :]
    mean = total * (1.0 / K)
    means[i, cols, :] = mean
    root_weight = obs[cols, i * 4 + 0, :]
    value = obs[cols, i * 4 + 1, :]
    index = obs[cols, i * 4 + 2, :].astype(jnp.int32)
    lane = jnp.bitwise_and(index, 127)
    tile = jnp.right_shift(index, 7)

    def pick(v):
        parts = [
            jnp.take_along_axis(v[:, 128 * t : 128 * (t + 1)], lane, axis=1, mode="promise_in_bounds") for t in range(4)
        ]
        return jnp.where(tile < 2, jnp.where(tile < 1, parts[0], parts[1]), jnp.where(tile < 3, parts[2], parts[3]))

    here = pl.ds(1 + g * GROUP, GROUP)
    for k in range(K):
        anomaly = x[k, i, cols, :] - mean
        x[k, i, cols, :] = anomaly
        stack[1 + i, here, k, :] = root_weight * pick(anomaly)
    stack[1 + i, here, K, :] = root_weight * (value - pick(mean))
    stack[1 + i, here, K + 1, :] = jnp.bitwise_and(index, SIDE * SIDE - 1).astype(F32)


def gram_column(stack, lhs, loc, gram, c, m, r):
    sub = lax.broadcasted_iota(jnp.int32, (8, 128), 0)
    point_row = jnp.right_shift(sub, 2)
    center_row = (jnp.bitwise_and(jnp.right_shift(sub, 1), 1) * 8).astype(F32) + 3.5
    center_col = (jnp.bitwise_and(sub, 1) * 8).astype(F32) + 3.5
    column = m * COLS + c - 1
    column_in = jnp.logical_and(column >= 0, column < BCOLS)
    for tr in range(ROWS + 2):
        cell = jnp.broadcast_to(stack[tr, c, pl.ds(K + 1, 1), :], (8, 128)).astype(jnp.int32)
        cell_row = jnp.right_shift(cell, 4).astype(F32)
        cell_col = jnp.bitwise_and(cell, 15).astype(F32)
        row = r * ROWS + tr - 1
        inside = jnp.logical_and(column_in, jnp.logical_and(row >= 0, row < BROWS))
        di = tr - 1 - point_row
        dy = (SIDE * di).astype(F32) + cell_row - center_row
        keep = jnp.logical_and(jnp.abs(di) <= 1, inside)
        lanes = pl.ds(tr * 128, 128)
        loc[pl.ds(pl.multiple_of(8 * c, 8), 8), lanes] = jnp.zeros((8, 128), F32)
        for e in (-1, 0, 1):
            dx = -SIDE * e + cell_col - center_col
            weight = jnp.exp((dy * dy + dx * dx) * (-1.0 / (2.0 * LOC_SCALE * LOC_SCALE)))
            loc[pl.ds(pl.multiple_of(8 * c + 16 + 8 * e, 8), 8), lanes] = jnp.where(keep, weight, 0.0)
        members = [stack[tr, c, pl.ds(8 * gj, 8), :] for gj in range(3)]
        pieces = []
        for k in range(K + 1):
            left = jnp.broadcast_to(stack[tr, c, pl.ds(k, 1), :], (8, 128))
            for gj in range(k // 8 if k < K else 0, 3):
                pieces.append(left * members[gj])
        pieces.append(jnp.zeros((8, 128), F32))
        for t in range(PAIRS // 16):
            both = jnp.concatenate(pieces[2 * t : 2 * t + 2], axis=0)
            high = both.astype(BF16)
            lhs[pl.ds(16 * t, 16), lanes] = high
            lhs[pl.ds(PAIRS + 16 * t, 16), lanes] = (both - high.astype(F32)).astype(BF16)
    weights = loc[pl.ds(24, 128), :]
    high = weights.astype(BF16)
    low = (weights - high.astype(F32)).astype(BF16)
    rhs = jnp.concatenate([high, low], axis=0)
    for half in range(2):
        rows = pl.ds(half * (PAIRS // 2), PAIRS // 2)
        dims = (((1,), (1,)), ((), ()))
        first = lax.dot_general(lhs[rows, :], rhs, dims, preferred_element_type=F32)
        second = lax.dot_general(
            lhs[pl.ds(PAIRS + half * (PAIRS // 2), PAIRS // 2), :], rhs, dims, preferred_element_type=F32
        )
        gram[rows, :] = gram[rows, :] + ((second[:, 128:] + second[:, :128]) + first[:, 128:] + first[:, :128])


def update_chunk(x, means, wts, result, g, i):
    cols = pl.ds(g * GROUP, GROUP)
    sub = lax.broadcasted_iota(jnp.int32, (8, 128), 0)
    lane = lax.broadcasted_iota(jnp.int32, (8, 128), 1)
    base = (g * GROUP + sub) * 8 + i * 4 + jnp.bitwise_and(jnp.right_shift(lane, 3), 1)
    for h in range(2):
        index = base + 2 * h

        def some(t, carry, h=h, index=index):
            acc = [[means[i, cols, pl.ds(128 * (2 * f + h), 128)] for f in range(2)] for _ in range(6)]
            for j in range(K):
                xs = [x[j, i, cols, pl.ds(128 * (2 * f + h), 128)] for f in range(2)]
                for u in range(6):
                    row = jnp.broadcast_to(wts[pl.ds(j * K + t * 6 + u, 1), :], (8, 128))
                    wv = jnp.take_along_axis(row, index, axis=1, mode="promise_in_bounds")
                    for f in range(2):
                        acc[u][f] = acc[u][f] + wv * xs[f]
            for u in range(6):
                for f in range(2):
                    result[t * 6 + u, i, cols, pl.ds(128 * (2 * f + h), 128)] = acc[u][f]
            return carry

        lax.fori_loop(0, K // 6, some, 0)


def kernel(
    ens, packed, out,
    x, obs, stack, means, lhs, loc, gram, wts, y, z, mm, tmp, result,
    obs_send, obs_recv, in_send, in_recv, own_in, halo_send, halo_recv, out_send, out_recv, own_out,
):
    m = lax.axis_index("member")
    r = lax.axis_index("region")

    barrier = pltpu.get_barrier_semaphore()
    around = [dev(m + d, r) for d in range(1, NM)] + [dev(m, r + d) for d in range(1, NR)]
    around += [dev(m + a, r + b) for a in (-1, 1) for b in (-1, 1)]
    for device in around:
        pl.semaphore_signal(barrier, inc=1, device_id=device, device_id_type=MESH)
    pl.semaphore_wait(barrier, len(around))

    def obs_copy(d):
        other = lax.rem(r + d, NR)
        return remote(packed.at[other], obs.at[r], obs_send.at[d], obs_recv.at[d], (m, other))

    for d in range(1, NR):
        obs_copy(d).start()

    def in_copy(q, d):
        g, i = CHUNKS[q]
        other = lax.rem(m + d, NM)
        src = ens.at[:, i, pl.ds(pl.multiple_of(other * COLS + g * GROUP, GROUP), GROUP), :]
        dst = x.at[pl.ds(m * MINE, MINE), i, pl.ds(g * GROUP, GROUP), :]
        return remote(src, dst, in_send.at[q, d], in_recv.at[q, d], (other, r))

    def own_copy(q):
        g, i = CHUNKS[q]
        src = ens.at[:, i, pl.ds(pl.multiple_of(m * COLS + g * GROUP, GROUP), GROUP), :]
        dst = x.at[pl.ds(m * MINE, MINE), i, pl.ds(g * GROUP, GROUP), :]
        return pltpu.make_async_copy(src, dst, own_in.at[q])

    for q in range(len(CHUNKS)):
        for d in range(1, NM):
            in_copy(q, d).start()
        own_copy(q).start()

    obs[r] = packed[r]
    loc[...] = jnp.zeros_like(loc)
    gram[...] = jnp.zeros_like(gram)
    for d in range(1, NR):
        obs_copy(d).wait_recv()

    def row_halo(g, i):
        where = pl.ds(1 + g * GROUP, GROUP)
        to = 3 if i == 0 else 0
        n = 2 * g + i
        return remote(
            stack.at[1 + i, where], stack.at[to, where], halo_send.at[n], halo_recv.at[n], dev(m, r + (-1 if i == 0 else 1))
        )

    def side_halo(g, n):
        col, to, a = (1, COLS + 1, -1) if g == 0 else (COLS, 0, 1)
        if n == 0:
            src, dst, b = stack.at[pl.ds(1, 2), col], stack.at[pl.ds(1, 2), to], 0
        elif n == 1:
            src, dst, b = stack.at[1, col], stack.at[3, to], -1
        else:
            src, dst, b = stack.at[2, col], stack.at[0, to], 1
        s = 4 + 3 * g + n
        return remote(src, dst, halo_send.at[s], halo_recv.at[s], dev(m + a, r + b))

    halos = []
    for q, (g, i) in enumerate(CHUNKS):
        own_copy(q).wait()
        for d in range(1, NM):
            in_copy(q, d).wait_recv()
        gather_chunk(x, obs, stack, means, g, i)
        new = [row_halo(g, i)]
        if i == ROWS - 1:
            new += [side_halo(g, n) for n in range(3)]
        for copy in new:
            copy.start()
        halos += new
    for copy in halos:
        copy.wait_recv()

    def column(c, carry):
        gram_column(stack, lhs, loc, gram, c, m, r)
        return carry

    lax.fori_loop(0, COLS + 2, column, 0)
    newton_schulz(gram, wts, y, z, mm, tmp)

    def out_copy(q, d):
        g, i = CHUNKS[q]
        other = lax.rem(m + d, NM)
        src = result.at[pl.ds(other * MINE, MINE), i, pl.ds(g * GROUP, GROUP), :]
        dst = out.at[:, i, pl.ds(pl.multiple_of(m * COLS + g * GROUP, GROUP), GROUP), :]
        return remote(src, dst, out_send.at[q, d], out_recv.at[q, d], (other, r))

    def keep_copy(q):
        g, i = CHUNKS[q]
        src = result.at[pl.ds(m * MINE, MINE), i, pl.ds(g * GROUP, GROUP), :]
        dst = out.at[:, i, pl.ds(pl.multiple_of(m * COLS + g * GROUP, GROUP), GROUP), :]
        return pltpu.make_async_copy(src, dst, own_out.at[q])

    for q, (g, i) in enumerate(CHUNKS):
        update_chunk(x, means, wts, result, g, i)
        for d in range(1, NM):
            out_copy(q, d).start()
        keep_copy(q).start()

    for d in range(1, NR):
        obs_copy(d).wait_send()
    for copy in halos:
        copy.wait_send()
    for q in range(len(CHUNKS)):
        for d in range(1, NM):
            in_copy(q, d).wait_send()
            out_copy(q, d).wait_send()
            out_copy(q, d).wait_recv()
        keep_copy(q).wait()


def local(ensemble, obs_value, obs_error, obs_index, obs_count):
    slot = lax.broadcasted_iota(jnp.int32, obs_index.shape, 2)
    live = jnp.where(slot < obs_count[:, :, None], 1.0, 0.0).astype(F32)
    root_weight = jnp.sqrt(live / obs_error)
    packed = jnp.concatenate([root_weight, obs_value, obs_index.astype(F32), jnp.zeros_like(obs_value)], axis=1)
    packed = packed.reshape(NR, 4 * ROWS, OBS)
    dma = pltpu.SemaphoreType.DMA
    n = len(CHUNKS)
    square = pltpu.VMEM((K * K, 128), F32)
    return pl.pallas_call(
        kernel,
        out_shape=jax.ShapeDtypeStruct(ensemble.shape, F32),
        in_specs=[pl.BlockSpec(memory_space=pl.ANY), pl.BlockSpec(memory_space=pltpu.VMEM)],
        out_specs=pl.BlockSpec(memory_space=pl.ANY),
        scratch_shapes=[
            pltpu.VMEM((K, ROWS, COLS, VALS), F32),
            pltpu.VMEM((COLS, 4 * ROWS, OBS), F32),
            pltpu.VMEM((ROWS + 2, COLS + 2, STACK, OBS), F32),
            pltpu.VMEM((ROWS, COLS, VALS), F32),
            pltpu.VMEM((2 * PAIRS, 512), BF16),
            pltpu.VMEM((168, 512), F32),
            pltpu.VMEM((PAIRS, 128), F32),
            square, square, square, square, square,
            pltpu.VMEM((K, ROWS, COLS, VALS), F32),
            dma((NR,)), dma((NR,)), dma((n, NM)), dma((n, NM)), dma((n,)),
            dma((10,)), dma((10,)), dma((n, NM)), dma((n, NM)), dma((n,)),
        ],
        compiler_params=pltpu.CompilerParams(collective_id=0, has_side_effects=True),
    )(ensemble, packed)


def solution(mesh):
    return jax.shard_map(
        local,
        mesh=mesh,
        in_specs=(
            P("member", "region", None, None),
            P(None, ("member", "region"), None),
            P(None, ("member", "region"), None),
            P(None, ("member", "region"), None),
            P(None, ("member", "region")),
        ),
        out_specs=P("member", "region", None, None),
        check_vma=False,
    )
```

time: 296 us -> 81.6 us (0.28)
  matrix products: 146 us -> 0 us
  Pallas kernels: 0 us -> 75.5 us
  blocking collectives: 52.4 us -> 0 us
  waiting for transfers between devices: 34.2 us -> 0 us
  local copies, waits for them, and re-layouts: 30.4 us -> 2.77 us
  starting transfers between devices: 20.4 us -> 0 us
  other arithmetic: 9.16 us -> 2.98 us
    dot_general x178 -> x0, matrix products: 146 us -> none  [the longest x136 62 us: batch_product(): jnp.einsum('...ij,...jk->...ik', left, right, precision=lax.Precision.HIG...]
    pallas_call x0 -> x1, Pallas kernels: none -> 75.5 us  [local(): pl.pallas_call(kernel, out_shape=jax.ShapeDtypeStruct(ensemble.shape, F32...]
    all_to_all x2 -> x0, blocking collectives: 52.4 us -> none  [the longest x1 29.3 us: local(): lax.all_to_all(by_rows, 'member', split_axis=0, concat_axis=2, tiled=True)]
    all_to_all x1 -> x0, waiting for transfers between devices: 23.9 us -> none  [exchange_both(): lax.all_to_all(blocks, axis, split_axis=0, concat_axis=0, tiled=True)]
    all_to_all x1 -> x0, starting transfers between devices: 11.5 us -> none  [exchange_both(): lax.all_to_all(blocks, axis, split_axis=0, concat_axis=0, tiled=True)]
    ppermute x2 -> x0, waiting for transfers between devices: 10.3 us -> none  [the longest x1 6.8 us: padded_2(): lax.ppermute(first, axis, [(b, a) for a, b in up])]
    dynamic_slice x16 -> x0, local copies, waits for them, and re-layouts: 10.2 us -> none  [one_group(): part_anom = lax.dynamic_slice_in_dim(anomaly, first_row_index, row_span, 1)]
    ppermute x2 -> x0, starting transfers between devices: 8.88 us -> none  [the longest x1 6.01 us: padded_2(): lax.ppermute(first, axis, [(b, a) for a, b in up])]
  transfers between devices with their start and end apart: 3 -> 0, of which waited for: 3 -> 0; matrix products, arithmetic and copies ran while one was open for 0% -> 0% of each run, Pallas kernels for 0% -> 0%
where the time goes in v1:
time: 81.6 us; the launch traced here: 81.3 us
  Pallas kernels  75.5 us (93%)
  other arithmetic  2.98 us (4%)
  local copies, waits for them, and re-layouts  2.77 us (3%)
    pallas_call x1, Pallas kernels, local(): pl.pallas_call(kernel, out_shape=jax.ShapeDtypeStruct(ensemble.shape, F32...  75.5 us
    unnamed x1, local copies, waits for them, and re-layouts  2.76 us

profile of v1, /device:TPU:1, one launch (start us, length us, event | category | flops | bytes accessed | tf_op | source)
XLA Modules:
  0.0 81.3 jit_solution(13388787858969620483)
XLA Ops:
  0.0 0.8 %fusion.1 = f32[32,1,128]{2,1,0:T(1,128)S(1)} fusion(f32[32,1,128]{2,1,0:T(1,128)} %param.7, s32[32]{0:T(128)} %bitcast.3), kind=kLoop, calls=%fused_computation.3 | loop fusion | flops 12288 | bytes 32896 | tf_op jit(solution)/shard_map/sqrt | solution.py:368
  0.8 0.7 convert_element_type.3
  1.6 1.4 %pad_maximum_fusion = f32[32,4,128]{2,1,0:T(4,128)} fusion(f32[32,1,128]{2,1,0:T(1,128)S(1)} %broadcast_in_dim.11, f32[32,1,128]{2,1,0:T(1,128)S(1)} %convert_element_type.3, f32[32,1,128]{2,1,0:T(1,128)} %param.6, f32[32,1,128]{2,1,0:T(1,128)S(1)} %fusion.1), kind=kLoop, calls=%fused_computation | loop fusion | flops 49152 | bytes 131072 | tf_op jit(solution)/shard_map/concatenate | solution.py:369
  3.0 75.5 %shard_map.58 = f32[3,2,128,512]{3,2,1,0:T(8,128)} custom-call(f32[3,2,128,512]{3,2,1,0:T(8,128)} %ens.1, f32[16,8,128]{2,1,0:T(8,128)} %bitcast.2), custom_call_target="tpu_custom_call" | custom-call | tf_op jit(solution)/shard_map/pallas_call | solution.py:374
  78.5 2.8 %copy.7 = f32[3,2,128,512]{3,2,1,0:T(8,128)} copy(f32[3,2,128,512]{3,2,1,0:T(8,128)} %shard_map.58) | data formatting | bytes 3145728
  (1 shorter events, 0.0 us)

commit v2 on v1

v2 whole, which is shorter than its diff:
```python
import functools
import math

import jax
import jax.numpy as jnp
from jax import lax
from jax.experimental import pallas as pl
from jax.experimental.pallas import tpu as pltpu
from jax.sharding import PartitionSpec as P

MESH = pl.DeviceIdType.MESH
F32 = jnp.float32
BF16 = jnp.bfloat16

SIDE = 16
OBS = 128
NS_ITERS = 6
VALS = 512
K = 24
BROWS = 32
BCOLS = 128
LOC_SCALE = 12.0
INFLATION_FACTOR = 1.1
NM = 8
NR = 16
MINE = K // NM
ROWS = BROWS // NR
COLS = BCOLS // NM
GROUP = 8
CHUNKS = [(g, i) for g in range(COLS // GROUP) for i in range(ROWS)]
STACK = 32
PAIRS = 52 * 8


def pair_row(k, group):
    first = k // 8
    return (0, 192, 320)[first] + (k % 8) * 8 * (3 - first) + 8 * (group - first)


DRIVE = 384


def dev(m, r):
    return (lax.rem(m + NM, NM), lax.rem(r + NR, NR))


def remote(src, dst, send, recv, device):
    return pltpu.make_async_remote_copy(
        src_ref=src, dst_ref=dst, send_sem=send, recv_sem=recv, device_id=device, device_id_type=MESH
    )


def tri_product(dst, a, b, post):
    for ga, height in ((0, 4), (1, 4), (2, 8)):
        groups = list(range(ga, 3))
        for first in range(8 * ga, 8 * ga + 8, height):
            acc = [[None] * len(groups) for _ in range(height)]
            for k in range(K):
                bv = [b[pl.ds(k * K + 8 * gj, 8), :] for gj in groups]
                for u in range(height):
                    av = jnp.broadcast_to(a[pl.ds((first + u) * K + k, 1), :], (8, 128))
                    for n in range(len(groups)):
                        term = av * bv[n]
                        acc[u][n] = term if acc[u][n] is None else acc[u][n] + term
            for u in range(height):
                for n, gj in enumerate(groups):
                    dst[pl.ds((first + u) * K + 8 * gj, 8), :] = post(acc[u][n], first + u, gj)
    fill_lower(dst)


def fill_lower(dst):
    for i in range(8, K):
        for gj in range(i // 8):
            dst[pl.ds(i * K + 8 * gj, 8), :] = dst[pl.ds(8 * gj * K + i, 8, stride=K), :]


def unit(i, gj):
    if i // 8 != gj:
        return jnp.zeros((8, 128), F32)
    return jnp.where(lax.broadcasted_iota(jnp.int32, (8, 128), 0) == i % 8, 1.0, 0.0).astype(F32)


def same(v, i, gj):
    return v


def newton_schulz(gram, wts, p, s, t, z, rest):
    square = jnp.zeros((8, 128), F32)
    for k in range(K):
        for gj in range(k // 8, 3):
            v = gram[pl.ds(pair_row(k, gj), 8), :] + (K - 1) / INFLATION_FACTOR * unit(k, gj)
            p[pl.ds(k * K + 8 * gj, 8), :] = v
            square = square + v * v * (1.0 if gj == k // 8 else 2.0)
    norm = jnp.sqrt(jnp.sum(square, axis=0, keepdims=True))
    inv_norm = 1.0 / norm
    for k in range(K):
        for gj in range(k // 8, 3):
            rows = pl.ds(k * K + 8 * gj, 8)
            p[rows, :] = p[rows, :] * inv_norm
    fill_lower(p)

    def square_of(v, i, gj):
        rows = pl.ds(i * K + 8 * gj, 8)
        rest[rows, :] = 1.6875 * unit(i, gj) - 0.5625 * p[rows, :] + 0.0625 * v
        return v

    def factor_of(v, i, gj):
        return v + (2.25 * unit(i, gj) - 2.4375 * p[pl.ds(i * K + 8 * gj, 8), :])

    def factor(dst):
        tri_product(s, p, p, square_of)
        fill_lower(rest)
        tri_product(dst, s, rest, factor_of)

    factor(z)
    tri_product(t, p, z, same)
    tri_product(p, t, z, same)
    factor(t)
    tri_product(s, p, t, same)
    tri_product(p, s, t, same)
    tri_product(wts, z, t, same)
    factor(t)
    tri_product(z, wts, t, same)
    scale = 1.0 / jnp.sqrt(norm)

    def apply(vector):
        acc = [jnp.zeros((8, 128), F32) for _ in range(3)]
        for k in range(K):
            row = vector[k // 8][k % 8 : k % 8 + 1, :]
            for gj in range(3):
                acc[gj] = acc[gj] + z[pl.ds(k * K + 8 * gj, 8), :] * row
        return [v * scale for v in acc]

    drive = [gram[pl.ds(DRIVE + 8 * gj, 8), :] for gj in range(3)]
    mean_w = apply(apply(drive))
    root = scale * math.sqrt(K - 1)
    for j in range(K):
        row = mean_w[j // 8][j % 8 : j % 8 + 1, :]
        for gj in range(3):
            rows = pl.ds(j * K + 8 * gj, 8)
            wts[rows, :] = z[rows, :] * root + row


def gather_chunk(x, obs, stack, means, g, i):
    cols = pl.ds(g * GROUP, GROUP)
    total = x[0, i, cols, :]
    for k in range(1, K):
        total = total + x[k, i, cols, :]
    mean = total * (1.0 / K)
    means[i, cols, :] = mean
    root_weight = obs[cols, i * 4 + 0, :]
    value = obs[cols, i * 4 + 1, :]
    index = obs[cols, i * 4 + 2, :].astype(jnp.int32)
    lane = jnp.bitwise_and(index, 127)
    tile = jnp.right_shift(index, 7)

    def pick(v):
        parts = [
            jnp.take_along_axis(v[:, 128 * t : 128 * (t + 1)], lane, axis=1, mode="promise_in_bounds") for t in range(4)
        ]
        return jnp.where(tile < 2, jnp.where(tile < 1, parts[0], parts[1]), jnp.where(tile < 3, parts[2], parts[3]))

    here = pl.ds(1 + g * GROUP, GROUP)
    for k in range(K):
        anomaly = x[k, i, cols, :] - mean
        x[k, i, cols, :] = anomaly
        stack[1 + i, here, k, :] = root_weight * pick(anomaly)
    stack[1 + i, here, K, :] = root_weight * (value - pick(mean))
    stack[1 + i, here, K + 1, :] = jnp.bitwise_and(index, SIDE * SIDE - 1).astype(F32)


def gram_blocks(stack, lhs, loc, gram, blocks, m, r):
    sub = lax.broadcasted_iota(jnp.int32, (8, 128), 0)
    point_row = jnp.right_shift(sub, 2)
    center_row = (jnp.bitwise_and(jnp.right_shift(sub, 1), 1) * 8).astype(F32) + 3.5
    center_col = (jnp.bitwise_and(sub, 1) * 8).astype(F32) + 3.5
    zero = jnp.zeros((8, 128), F32)
    blank = jnp.zeros((16, 128), BF16)
    for n, (tr, c) in enumerate(blocks):
        lanes = pl.ds(n * 128, 128)
        cell = jnp.broadcast_to(stack[tr, c, pl.ds(K + 1, 1), :], (8, 128)).astype(jnp.int32)
        cell_row = jnp.right_shift(cell, 4).astype(F32)
        cell_col = jnp.bitwise_and(cell, 15).astype(F32)
        row = r * ROWS + tr - 1
        column = m * COLS + c - 1
        inside = jnp.logical_and(jnp.logical_and(column >= 0, column < BCOLS), jnp.logical_and(row >= 0, row < BROWS))
        di = tr - 1 - point_row
        dy = (SIDE * di).astype(F32) + cell_row - center_row
        keep = jnp.logical_and(jnp.abs(di) <= 1, inside)
        reach = {}
        for e in (-1, 0, 1):
            if 0 <= c - 1 + e < COLS:
                dx = cell_col - center_col - float(SIDE * e)
                weight = jnp.exp((dy * dy + dx * dx) * (-1.0 / (2.0 * LOC_SCALE * LOC_SCALE)))
                reach[c - 1 + e] = jnp.where(keep, weight, 0.0)
        for tile in range(COLS // 2):
            if 2 * tile in reach or 2 * tile + 1 in reach:
                both = jnp.concatenate([reach.get(2 * tile, zero), reach.get(2 * tile + 1, zero)], axis=0)
                high = both.astype(BF16)
                low = (both - high.astype(F32)).astype(BF16)
            else:
                high = low = blank
            loc[pl.ds(16 * tile, 16), lanes] = high
            loc[pl.ds(128 + 16 * tile, 16), lanes] = low
        members = [stack[tr, c, pl.ds(8 * gj, 8), :] for gj in range(3)]
        pieces = []
        for k in range(K + 1):
            left = jnp.broadcast_to(stack[tr, c, pl.ds(k, 1), :], (8, 128))
            for gj in range(k // 8 if k < K else 0, 3):
                pieces.append(left * members[gj])
        pieces.append(zero)
        for t in range(PAIRS // 16):
            both = jnp.concatenate(pieces[2 * t : 2 * t + 2], axis=0)
            high = both.astype(BF16)
            lhs[pl.ds(16 * t, 16), lanes] = high
            lhs[pl.ds(PAIRS + 16 * t, 16), lanes] = (both - high.astype(F32)).astype(BF16)
    depth = pl.ds(0, 128 * len(blocks))
    dims = (((1,), (1,)), ((), ()))
    total = lax.dot_general(lhs[:, depth], loc[:, depth], dims, preferred_element_type=F32)
    high, low = total[:PAIRS], total[PAIRS:]
    gram[...] = gram[...] + ((low[:, 128:] + low[:, :128]) + high[:, 128:] + high[:, :128])


def update_members(x, means, wts, result, g, i, others):
    cols = pl.ds(pl.multiple_of(g * GROUP, GROUP), GROUP)
    sub = lax.broadcasted_iota(jnp.int32, (8, 128), 0)
    lane = lax.broadcasted_iota(jnp.int32, (8, 128), 1)
    base = (g * GROUP + sub) * 8 + i * 4 + jnp.bitwise_and(jnp.right_shift(lane, 3), 1)
    members = [other * MINE + u for other in others for u in range(MINE)]
    for h in range(2):
        index = base + 2 * h
        acc = [[means[i, cols, pl.ds(128 * (2 * f + h), 128)] for f in range(2)] for _ in members]
        for j in range(K):
            xs = [x[j, i, cols, pl.ds(128 * (2 * f + h), 128)] for f in range(2)]
            for u, k in enumerate(members):
                row = jnp.broadcast_to(wts[pl.ds(j * K + k, 1), :], (8, 128))
                wv = jnp.take_along_axis(row, index, axis=1, mode="promise_in_bounds")
                for f in range(2):
                    acc[u][f] = acc[u][f] + wv * xs[f]
        for u, k in enumerate(members):
            for f in range(2):
                result[k, i, cols, pl.ds(128 * (2 * f + h), 128)] = acc[u][f]


def kernel(
    ens, value_in, error_in, index_in, count, out,
    value, error, index, load,
    x, obs, packed, stack, means, lhs, loc, gram, wts, y, z, mm, tmp, rest, result,
    obs_send, obs_recv, in_send, in_recv, own_in, halo_send, halo_recv, out_send, out_recv, own_out,
):
    m = lax.axis_index("member")
    r = lax.axis_index("region")

    loads = [
        pltpu.make_async_copy(src, dst, load.at[n])
        for n, (src, dst) in enumerate(((value_in, value), (error_in, error), (index_in, index)))
    ]
    for copy in loads:
        copy.start()
    barrier = pltpu.get_barrier_semaphore()
    around = [dev(m + d, r) for d in range(1, NM)] + [dev(m, r + d) for d in range(1, NR)]
    around += [dev(m + a, r + b) for a in (-1, 1) for b in (-1, 1)]
    for device in around:
        pl.semaphore_signal(barrier, inc=1, device_id=device, device_id_type=MESH)
    for copy in loads:
        copy.wait()
    sub = lax.broadcasted_iota(jnp.int32, (8, OBS), 0)
    slot = lax.broadcasted_iota(jnp.int32, (8, OBS), 1)
    for n in range(BROWS // 8):
        rows = pl.ds(8 * n, 8)
        limit = jnp.zeros((8, OBS), jnp.int32)
        for u in range(8):
            limit = jnp.where(sub == u, count[0, 8 * n + u], limit)
        live = jnp.where(slot < limit, 1.0, 0.0).astype(F32)
        fields = (jnp.sqrt(live / error[rows, 0, :]), value[rows, 0, :], index[rows, 0, :].astype(F32))
        for f, field in enumerate(fields):
            for u in range(8):
                to = 8 * n + u
                packed[to // ROWS, to % ROWS * 4 + f, :] = field[u]
    pl.semaphore_wait(barrier, len(around))

    def obs_copy(d):
        other = lax.rem(r + d, NR)
        return remote(packed.at[other], obs.at[r], obs_send.at[d], obs_recv.at[d], (m, other))

    for d in range(1, NR):
        obs_copy(d).start()

    def in_copy(q, d):
        g, i = CHUNKS[q]
        other = lax.rem(m + d, NM)
        src = ens.at[:, i, pl.ds(pl.multiple_of(other * COLS + g * GROUP, GROUP), GROUP), :]
        dst = x.at[pl.ds(m * MINE, MINE), i, pl.ds(g * GROUP, GROUP), :]
        return remote(src, dst, in_send.at[q, d], in_recv.at[q, d], (other, r))

    def own_copy(q):
        g, i = CHUNKS[q]
        src = ens.at[:, i, pl.ds(pl.multiple_of(m * COLS + g * GROUP, GROUP), GROUP), :]
        dst = x.at[pl.ds(m * MINE, MINE), i, pl.ds(g * GROUP, GROUP), :]
        return pltpu.make_async_copy(src, dst, own_in.at[q])

    def send_in(q):
        for d in range(1, NM):
            in_copy(q, d).start()
        own_copy(q).start()

    send_in(0)
    send_in(1)
    obs[r] = packed[r]
    gram[...] = jnp.zeros_like(gram)
    for d in range(1, NR):
        obs_copy(d).wait_recv()

    def row_halo(g, i):
        where = pl.ds(1 + g * GROUP, GROUP)
        to = 3 if i == 0 else 0
        n = 2 * g + i
        return remote(
            stack.at[1 + i, where], stack.at[to, where], halo_send.at[n], halo_recv.at[n], dev(m, r + (-1 if i == 0 else 1))
        )

    def side_halo(g, n):
        col, to, a = (1, COLS + 1, -1) if g == 0 else (COLS, 0, 1)
        if n == 0:
            src, dst, b = stack.at[pl.ds(1, 2), col], stack.at[pl.ds(1, 2), to], 0
        elif n == 1:
            src, dst, b = stack.at[1, col], stack.at[3, to], -1
        else:
            src, dst, b = stack.at[2, col], stack.at[0, to], 1
        s = 4 + 3 * g + n
        return remote(src, dst, halo_send.at[s], halo_recv.at[s], dev(m + a, r + b))

    halos = []

    def arrive(q):
        g, i = CHUNKS[q]
        own_copy(q).wait()
        for d in range(1, NM):
            in_copy(q, d).wait_recv()
        gather_chunk(x, obs, stack, means, g, i)
        new = [row_halo(g, i)]
        if i == ROWS - 1:
            new += [side_halo(g, n) for n in range(3)]
        for copy in new:
            copy.start()
        halos.extend(new)
        if q + 2 < len(CHUNKS):
            send_in(q + 2)

    def add(blocks):
        gram_blocks(stack, lhs, loc, gram, blocks, m, r)

    def own(q):
        g, i = CHUNKS[q]
        return [(1 + i, 1 + g * GROUP + c) for c in range(GROUP)]

    def beyond(q):
        g, i = CHUNKS[q]
        return [(3 if i == 0 else 0, 1 + g * GROUP + c) for c in range(GROUP)]

    arrive(0)
    arrive(1)
    row_halo(*CHUNKS[0]).wait_recv()
    add(own(0) + beyond(0))
    arrive(2)
    row_halo(*CHUNKS[1]).wait_recv()
    add(own(1) + beyond(1))
    arrive(3)
    row_halo(*CHUNKS[2]).wait_recv()
    for n in range(3):
        side_halo(0, n).wait_recv()
    add(own(2) + beyond(2) + own(3) + [(tr, COLS + 1) for tr in range(4)])
    row_halo(*CHUNKS[3]).wait_recv()
    for n in range(3):
        side_halo(1, n).wait_recv()
    add(beyond(3) + [(tr, 0) for tr in range(4)])
    newton_schulz(gram, wts, y, z, mm, tmp, rest)

    def out_copy(q, d):
        g, i = q // ROWS, q % ROWS
        other = lax.rem(m + d, NM)
        src = result.at[pl.ds(other * MINE, MINE), i, pl.ds(pl.multiple_of(g * GROUP, GROUP), GROUP), :]
        dst = out.at[:, i, pl.ds(pl.multiple_of(m * COLS + g * GROUP, GROUP), GROUP), :]
        return remote(src, dst, out_send.at[q, d], out_recv.at[q, d], (other, r))

    def keep_copy(q):
        g, i = q // ROWS, q % ROWS
        src = result.at[pl.ds(m * MINE, MINE), i, pl.ds(pl.multiple_of(g * GROUP, GROUP), GROUP), :]
        dst = out.at[:, i, pl.ds(pl.multiple_of(m * COLS + g * GROUP, GROUP), GROUP), :]
        return pltpu.make_async_copy(src, dst, own_out.at[q])

    def chunk_out(q, carry):
        for pair in ((1, 2), (3, 4), (5, 6), (7, 0)):
            update_members(x, means, wts, result, q // ROWS, q % ROWS, [lax.rem(m + d, NM) for d in pair])
            for d in pair:
                (out_copy(q, d) if d else keep_copy(q)).start()
        return carry

    lax.fori_loop(0, len(CHUNKS), chunk_out, 0)

    for d in range(1, NR):
        obs_copy(d).wait_send()
    for copy in halos:
        copy.wait_send()
    for q in range(len(CHUNKS)):
        for d in range(1, NM):
            in_copy(q, d).wait_send()
            out_copy(q, d).wait_send()
            out_copy(q, d).wait_recv()
        keep_copy(q).wait()


def local(ensemble, obs_value, obs_error, obs_index, obs_count):
    dma = pltpu.SemaphoreType.DMA
    n = len(CHUNKS)
    square = pltpu.VMEM((K * K, 128), F32)
    return pl.pallas_call(
        kernel,
        out_shape=jax.ShapeDtypeStruct(ensemble.shape, F32),
        in_specs=[pl.BlockSpec(memory_space=pltpu.MemorySpace.HBM)] * 4 + [pl.BlockSpec(memory_space=pltpu.SMEM)],
        out_specs=pl.BlockSpec(memory_space=pl.ANY),
        scratch_shapes=[
            pltpu.VMEM((BROWS, 1, OBS), F32), pltpu.VMEM((BROWS, 1, OBS), F32), pltpu.VMEM((BROWS, 1, OBS), jnp.int32), dma((3,)),
            pltpu.VMEM((K, ROWS, COLS, VALS), F32),
            pltpu.VMEM((COLS, 4 * ROWS, OBS), F32),
            pltpu.VMEM((NR, 4 * ROWS, OBS), F32),
            pltpu.VMEM((ROWS + 2, COLS + 2, STACK, OBS), F32),
            pltpu.VMEM((ROWS, COLS, VALS), F32),
            pltpu.VMEM((2 * PAIRS, 28 * 128), BF16),
            pltpu.VMEM((256, 28 * 128), BF16),
            pltpu.VMEM((PAIRS, 128), F32),
            square, square, square, square, square, square,
            pltpu.VMEM((K, ROWS, COLS, VALS), F32),
            dma((NR,)), dma((NR,)), dma((n, NM)), dma((n, NM)), dma((n,)),
            dma((10,)), dma((10,)), dma((n, NM)), dma((n, NM)), dma((n,)),
        ],
        compiler_params=pltpu.CompilerParams(collective_id=0, has_side_effects=True),
    )(ensemble, obs_value, obs_error, obs_index, obs_count.reshape(1, BROWS))


def solution(mesh):
    return jax.shard_map(
        local,
        mesh=mesh,
        in_specs=(
            P("member", "region", None, None),
            P(None, ("member", "region"), None),
            P(None, ("member", "region"), None),
            P(None, ("member", "region"), None),
            P(None, ("member", "region")),
        ),
        out_specs=P("member", "region", None, None),
        check_vma=False,
    )
```

time: 81.6 us -> 66.1 us (0.81)
  Pallas kernels: 75.5 us -> 63.1 us
  other arithmetic: 2.98 us -> 0 us
    pallas_call x1, Pallas kernels: 75.5 us -> 63.1 us  [local(): pl.pallas_call(kernel, out_shape=jax.ShapeDtypeStruct(ensemble.shape, F32...]
    concatenate x1 -> x0, other arithmetic: 1.42 us -> none  [local(): jnp.concatenate([root_weight, obs_value, obs_index.astype(F32), jnp.zeros...]
    sqrt x1 -> x0, other arithmetic: 0.83 us -> none  [local(): root_weight = jnp.sqrt(live / obs_error)]
where the time goes in v2:
time: 66.1 us; the launch traced here: 65.8 us
  Pallas kernels  63.1 us (95%)
  local copies, waits for them, and re-layouts  2.76 us (4%)
    pallas_call x1, Pallas kernels, local(): pl.pallas_call(kernel, out_shape=jax.ShapeDtypeStruct(ensemble.shape, F32...  63.1 us
    unnamed x1, local copies, waits for them, and re-layouts  2.76 us

profile of v2, /device:TPU:1, one launch (start us, length us, event | category | flops | bytes accessed | tf_op | source)
XLA Modules:
  0.0 65.8 jit_solution(7444032108430100082)
XLA Ops:
  0.0 63.1 %shard_map.55 = f32[3,2,128,512]{3,2,1,0:T(8,128)} custom-call(f32[3,2,128,512]{3,2,1,0:T(8,128)} %ens.1, f32[32,1,128]{2,1,0:T(1,128)} %value_in.1, f32[32,1,128]{2,1,0:T(1,128)} %error_in.1, s32[32,1,128]{2,1,0:T(1,128)} %index_in.1, s32[1,32]{1,0:T(1,128)} %bitcast.1), custom_call_target="tpu_custom_call" | custom-call | tf_op jit(solution)/shard_map/pallas_call | solution.py:417
  63.1 2.8 %copy.7 = f32[3,2,128,512]{3,2,1,0:T(8,128)} copy(f32[3,2,128,512]{3,2,1,0:T(8,128)} %shard_map.55) | data formatting | bytes 3145728

commit v3 on v2

v3 whole, which is shorter than its diff:
```python
import functools
import math

import jax
import jax.numpy as jnp
from jax import lax
from jax.experimental import pallas as pl
from jax.experimental.pallas import tpu as pltpu
from jax.sharding import PartitionSpec as P

MESH = pl.DeviceIdType.MESH
F32 = jnp.float32
BF16 = jnp.bfloat16

SIDE = 16
OBS = 128
NS_ITERS = 6
VALS = 512
K = 24
BROWS = 32
BCOLS = 128
LOC_SCALE = 12.0
INFLATION_FACTOR = 1.1
NM = 8
NR = 16
MINE = K // NM
ROWS = BROWS // NR
COLS = BCOLS // NM
GROUP = 8
CHUNKS = [(g, i) for g in range(COLS // GROUP) for i in range(ROWS)]
AT = GROUP - 1
TERMS = [(a, b, d) for a in range(3) for b in range(a, 3) for d in range(8 if b > a else 5)]
DRIVE = 8 * len(TERMS)
PAIRS = DRIVE + K
DEEP = 8


def dev(m, r):
    return (lax.rem(m + NM, NM), lax.rem(r + NR, NR))


def remote(src, dst, send, recv, device):
    return pltpu.make_async_remote_copy(
        src_ref=src, dst_ref=dst, send_sem=send, recv_sem=recv, device_id=device, device_id_type=MESH
    )


def tri_product(dst, a, b, post):
    for ga, height in ((0, 4), (1, 4), (2, 8)):
        groups = list(range(ga, 3))
        for first in range(8 * ga, 8 * ga + 8, height):
            acc = [[None] * len(groups) for _ in range(height)]
            for k in range(K):
                bv = [b[pl.ds(k * K + 8 * gj, 8), :] for gj in groups]
                for u in range(height):
                    av = jnp.broadcast_to(a[pl.ds((first + u) * K + k, 1), :], (8, 128))
                    for n in range(len(groups)):
                        term = av * bv[n]
                        acc[u][n] = term if acc[u][n] is None else acc[u][n] + term
            for u in range(height):
                for n, gj in enumerate(groups):
                    dst[pl.ds((first + u) * K + 8 * gj, 8), :] = post(acc[u][n], first + u, gj)
    fill_lower(dst)


def fill_lower(dst):
    for i in range(8, K):
        for gj in range(i // 8):
            dst[pl.ds(i * K + 8 * gj, 8), :] = dst[pl.ds(8 * gj * K + i, 8, stride=K), :]


def unit(i, gj):
    if i // 8 != gj:
        return jnp.zeros((8, 128), F32)
    return jnp.where(lax.broadcasted_iota(jnp.int32, (8, 128), 0) == i % 8, 1.0, 0.0).astype(F32)


def same(v, i, gj):
    return v


def newton_schulz(gram, wts, p, s, t, z, rest):
    square = jnp.zeros((8, 128), F32)
    for ga in range(3):
        for gb in range(ga, 3):
            base = 8 * TERMS.index((ga, gb, 0))
            source, start = gram, base
            if ga == gb:
                source, start = rest, 64 * ga
                for d in range(8):
                    v = gram[pl.ds(base + 8 * min(d, 8 - d), 8), :]
                    rest[pl.ds(start + 8 * d, 8), :] = pltpu.roll(v, 8 - d, 0) if d > 4 else v
            for u in range(8):
                k = 8 * ga + u
                v = source[pl.ds(start + u, 8, stride=8), :]
                v = pltpu.roll(v, u, 0) if u else v
                if ga == gb:
                    v = v + (K - 1) / INFLATION_FACTOR * unit(k, gb)
                p[pl.ds(k * K + 8 * gb, 8), :] = v
                square = square + v * v * (1.0 if ga == gb else 2.0)
    norm = jnp.sqrt(jnp.sum(square, axis=0, keepdims=True))
    inv_norm = 1.0 / norm
    for k in range(K):
        for gj in range(k // 8, 3):
            rows = pl.ds(k * K + 8 * gj, 8)
            p[rows, :] = p[rows, :] * inv_norm
    fill_lower(p)

    def square_of(v, i, gj):
        rows = pl.ds(i * K + 8 * gj, 8)
        rest[rows, :] = 1.6875 * unit(i, gj) - 0.5625 * p[rows, :] + 0.0625 * v
        return v

    def factor_of(v, i, gj):
        return v + (2.25 * unit(i, gj) - 2.4375 * p[pl.ds(i * K + 8 * gj, 8), :])

    def factor(dst):
        tri_product(s, p, p, square_of)
        fill_lower(rest)
        tri_product(dst, s, rest, factor_of)

    factor(z)
    tri_product(t, p, z, same)
    tri_product(p, t, z, same)
    factor(t)
    tri_product(s, p, t, same)
    tri_product(p, s, t, same)
    tri_product(wts, z, t, same)
    factor(t)
    tri_product(z, wts, t, same)
    scale = 1.0 / jnp.sqrt(norm)

    def apply(vector):
        acc = [jnp.zeros((8, 128), F32) for _ in range(3)]
        for k in range(K):
            row = vector[k // 8][k % 8 : k % 8 + 1, :]
            for gj in range(3):
                acc[gj] = acc[gj] + z[pl.ds(k * K + 8 * gj, 8), :] * row
        return [v * scale for v in acc]

    drive = [gram[pl.ds(DRIVE + 8 * gj, 8), :] for gj in range(3)]
    mean_w = apply(apply(drive))
    root = scale * math.sqrt(K - 1)
    for j in range(K):
        row = mean_w[j // 8][j % 8 : j % 8 + 1, :]
        for gj in range(3):
            rows = pl.ds(j * K + 8 * gj, 8)
            wts[rows, :] = z[rows, :] * root + row


def gather_group(mine, places, seen_out, m, g):
    for other in range(NM):
        cols = pl.ds(other * COLS + g * GROUP, GROUP)
        for i in range(ROWS):
            index = places[i, cols, :].astype(jnp.int32)
            lane = jnp.bitwise_and(index, 127)
            tile = jnp.right_shift(index, 7)
            for u in range(MINE):
                v = [
                    jnp.take_along_axis(mine[u, i, cols, pl.ds(128 * t, 128)], lane, axis=1, mode="promise_in_bounds")
                    for t in range(4)
                ]
                low, high = jnp.where(tile < 1, v[0], v[1]), jnp.where(tile < 3, v[2], v[3])
                seen_out[g, other, u, i] = jnp.where(tile < 2, low, high)


def stack_group(seen, obs, stack, extra, g):
    cols = pl.ds(g * GROUP, GROUP)
    here = pl.ds(1 + g * GROUP, GROUP)
    for i in range(ROWS):
        total = seen[g, 0, i]
        for k in range(1, K):
            total = total + seen[g, k, i]
        mean = total * (1.0 / K)
        root_weight = obs[cols, i * 4 + 0, :]
        for k in range(K):
            stack[1 + i, here, k, :] = root_weight * (seen[g, k, i] - mean)
        index = obs[cols, i * 4 + 2, :].astype(jnp.int32)
        extra[1 + i, 0, pl.ds((1 + g) * GROUP, GROUP), :] = root_weight * (obs[cols, i * 4 + 1, :] - mean)
        extra[1 + i, 1, pl.ds((1 + g) * GROUP, GROUP), :] = jnp.bitwise_and(index, SIDE * SIDE - 1).astype(F32)


def center_chunk(x, means, g, i):
    cols = pl.ds(pl.multiple_of(g * GROUP, GROUP), GROUP)
    for t in range(4):
        lanes = pl.ds(128 * t, 128)
        total = x[0, i, cols, lanes]
        for k in range(1, K):
            total = total + x[k, i, cols, lanes]
        mean = total * (1.0 / K)
        means[i, cols, lanes] = mean
        for k in range(K):
            x[k, i, cols, lanes] = x[k, i, cols, lanes] - mean


def gram_blocks(stack, extra, buffers, gram, blocks, m, r):
    sub = lax.broadcasted_iota(jnp.int32, (8, 128), 0)
    point_row = jnp.right_shift(sub, 2)
    center_row = (jnp.bitwise_and(jnp.right_shift(sub, 1), 1) * 8).astype(F32) + 3.5
    center_col = (jnp.bitwise_and(sub, 1) * 8).astype(F32) + 3.5
    zero = jnp.zeros((8, 128), F32)
    blank = jnp.zeros((16, 128), BF16)
    for n, (tr, c) in enumerate(blocks):
        lhs, loc = buffers[n // DEEP % 2]
        lanes = pl.ds(n % DEEP * 128, 128)
        cell = jnp.broadcast_to(extra[tr, 1, pl.ds(AT + c, 1), :], (8, 128)).astype(jnp.int32)
        cell_row = jnp.right_shift(cell, 4).astype(F32)
        cell_col = jnp.bitwise_and(cell, 15).astype(F32)
        row = r * ROWS + tr - 1
        column = m * COLS + c - 1
        inside = jnp.logical_and(jnp.logical_and(column >= 0, column < BCOLS), jnp.logical_and(row >= 0, row < BROWS))
        di = tr - 1 - point_row
        dy = (SIDE * di).astype(F32) + cell_row - center_row
        keep = jnp.logical_and(jnp.abs(di) <= 1, inside)
        reach = {}
        for e in (-1, 0, 1):
            if 0 <= c - 1 + e < COLS:
                dx = cell_col - center_col - float(SIDE * e)
                weight = jnp.exp((dy * dy + dx * dx) * (-1.0 / (2.0 * LOC_SCALE * LOC_SCALE)))
                reach[c - 1 + e] = jnp.where(keep, weight, 0.0)
        for tile in range(COLS // 2):
            if 2 * tile in reach or 2 * tile + 1 in reach:
                both = jnp.concatenate([reach.get(2 * tile, zero), reach.get(2 * tile + 1, zero)], axis=0)
                high = both.astype(BF16)
                low = (both - high.astype(F32)).astype(BF16)
            else:
                high = low = blank
            loc[pl.ds(16 * tile, 16), lanes] = high
            loc[pl.ds(128 + 16 * tile, 16), lanes] = low
        members = [stack[tr, c, pl.ds(8 * gj, 8), :] for gj in range(3)]
        turned = [[pltpu.roll(v, 8 - d, 0) if d else v for d in range(8)] for v in members]
        innovation = jnp.broadcast_to(extra[tr, 0, pl.ds(AT + c, 1), :], (8, 128))
        pieces = [members[ga] * turned[gb][d] for ga, gb, d in TERMS] + [innovation * v for v in members]
        for t in range(PAIRS // 16):
            both = jnp.concatenate(pieces[2 * t : 2 * t + 2], axis=0)
            high = both.astype(BF16)
            lhs[pl.ds(16 * t, 16), lanes] = high
            lhs[pl.ds(PAIRS + 16 * t, 16), lanes] = (both - high.astype(F32)).astype(BF16)
        if n % DEEP == DEEP - 1 or n == len(blocks) - 1:
            depth = pl.ds(0, 128 * (n % DEEP + 1))
            dims = (((1,), (1,)), ((), ()))
            high = lax.dot_general(lhs[pl.ds(0, PAIRS), depth], loc[:, depth], dims, preferred_element_type=F32)
            low = lax.dot_general(
                lhs[pl.ds(PAIRS, PAIRS), depth], loc[pl.ds(0, 128), depth], dims, preferred_element_type=F32
            )
            gram[...] = gram[...] + ((low + high[:, 128:]) + high[:, :128])


def update_members(x, means, wts, result, g, i, others):
    cols = pl.ds(pl.multiple_of(g * GROUP, GROUP), GROUP)
    sub = lax.broadcasted_iota(jnp.int32, (8, 128), 0)
    lane = lax.broadcasted_iota(jnp.int32, (8, 128), 1)
    base = (g * GROUP + sub) * 8 + i * 4 + jnp.bitwise_and(jnp.right_shift(lane, 3), 1)
    members = [other * MINE + u for other in others for u in range(MINE)]
    for h in range(2):
        index = base + 2 * h
        acc = [[means[i, cols, pl.ds(128 * (2 * f + h), 128)] for f in range(2)] for _ in members]
        for j in range(K):
            xs = [x[j, i, cols, pl.ds(128 * (2 * f + h), 128)] for f in range(2)]
            for u, k in enumerate(members):
                row = jnp.broadcast_to(wts[pl.ds(j * K + k, 1), :], (8, 128))
                wv = jnp.take_along_axis(row, index, axis=1, mode="promise_in_bounds")
                for f in range(2):
                    acc[u][f] = acc[u][f] + wv * xs[f]
        for u, k in enumerate(members):
            for f in range(2):
                result[k, i, cols, pl.ds(128 * (2 * f + h), 128)] = acc[u][f]


def kernel(
    ens, value_in, error_in, index_in, count_in, out,
    count,    value, error, index, load,
    x, obs, packed, stack, extra, means, lhs0, loc0, lhs1, loc1, mine, places, seen_out, seen, gram, wts, y, z, mm, tmp, rest, result,
    obs_send, obs_recv, in_send, in_recv, own_in, halo_send, halo_recv, out_send, out_recv, own_out, place_send, place_recv, seen_send, seen_recv,
):
    m = lax.axis_index("member")
    r = lax.axis_index("region")

    loads = [
        pltpu.make_async_copy(src, dst, load.at[n])
        for n, (src, dst) in enumerate(((value_in, value), (error_in, error), (index_in, index), (count_in, count), (ens, mine)))
    ]
    for copy in loads:
        copy.start()
    barrier = pltpu.get_barrier_semaphore()
    around = [dev(m + d, r) for d in range(1, NM)] + [dev(m, r + d) for d in range(1, NR)]
    around += [dev(m + a, r + b) for a in (-1, 1) for b in (-1, 1)]
    for device in around:
        pl.semaphore_signal(barrier, inc=1, device_id=device, device_id_type=MESH)
    for copy in loads[:4]:
        copy.wait()
    sub = lax.broadcasted_iota(jnp.int32, (8, OBS), 0)
    slot = lax.broadcasted_iota(jnp.int32, (8, OBS), 1)
    for n in range(BROWS // 8):
        rows = pl.ds(8 * n, 8)
        limit = jnp.zeros((8, OBS), jnp.int32)
        for u in range(8):
            limit = jnp.where(sub == u, count[0, 8 * n + u], limit)
        live = jnp.where(slot < limit, 1.0, 0.0).astype(F32)
        fields = (jnp.sqrt(live / error[rows, 0, :]), value[rows, 0, :], index[rows, 0, :].astype(F32))
        for f, field in enumerate(fields):
            for u in range(8):
                to = 8 * n + u
                packed[to // ROWS, to % ROWS * 4 + f, :] = field[u]
    pl.semaphore_wait(barrier, len(around))

    def obs_copy(d):
        other = lax.rem(r + d, NR)
        return remote(packed.at[other], obs.at[r], obs_send.at[0], obs_recv.at[0], (m, other))

    for d in range(1, NR):
        obs_copy(d).start()

    def in_copy(q, d):
        g, i = q // ROWS, q % ROWS
        other = lax.rem(m + d, NM)
        src = mine.at[:, i, pl.ds(pl.multiple_of(other * COLS + g * GROUP, GROUP), GROUP), :]
        dst = x.at[pl.ds(m * MINE, MINE), i, pl.ds(pl.multiple_of(g * GROUP, GROUP), GROUP), :]
        return remote(src, dst, in_send.at[q], in_recv.at[q], (other, r))

    def in_all(q):
        g, i = q // ROWS, q % ROWS
        part = x.at[pl.ds(0, K - MINE), i, pl.ds(pl.multiple_of(g * GROUP, GROUP), GROUP), :]
        return remote(part, part, in_send.at[q], in_recv.at[q], (m, r))

    def own_copy(q):
        g, i = q // ROWS, q % ROWS
        src = ens.at[:, i, pl.ds(pl.multiple_of(m * COLS + g * GROUP, GROUP), GROUP), :]
        dst = x.at[pl.ds(m * MINE, MINE), i, pl.ds(pl.multiple_of(g * GROUP, GROUP), GROUP), :]
        return pltpu.make_async_copy(src, dst, own_in.at[q])

    def send_in(q, part=range(NM)):
        for d in part:
            (in_copy(q, d) if d else own_copy(q)).start()

    loads[4].wait()
    send_in(0, (2, 6, 1, 7))
    obs[r] = packed[r]
    gram[...] = jnp.zeros_like(gram)
    obs_all = remote(packed.at[pl.ds(0, NR - 1)], obs.at[pl.ds(0, NR - 1)], obs_send.at[0], obs_recv.at[0], (m, r))
    obs_all.wait_recv()

    def place_copy(d):
        own = places.at[:, pl.ds(pl.multiple_of(m * COLS, COLS), COLS), :]
        return remote(own, own, place_send.at[0], place_recv.at[0], (lax.rem(m + d, NM), r))

    def seen_copy(g, d):
        other = lax.rem(m + d, NM)
        dst = seen.at[g, pl.ds(m * MINE, MINE)]
        return remote(seen_out.at[g, other], dst, seen_send.at[g], seen_recv.at[g], (other, r))

    def seen_all(g):
        part = seen.at[g, pl.ds(0, K - MINE)]
        return remote(part, part, seen_send.at[g], seen_recv.at[g], (m, r))

    for i in range(ROWS):
        for g in range(2):
            cols = pl.ds(pl.multiple_of(m * COLS + g * GROUP, GROUP), GROUP)
            places[i, cols, :] = obs[pl.ds(g * GROUP, GROUP), i * 4 + 2, :]
    for d in range(1, NM):
        place_copy(d).start()
    send_in(0, (3, 5, 4, 0))

    def halo_pair(src, dst, sem, device):
        return [remote(ref.at[a], ref.at[b], halo_send.at[sem], halo_recv.at[sem], device) for ref, a, b in zip((stack, extra), src, dst)]

    def row_halo(g, i):
        to = 3 if i == 0 else 0
        where, wide = pl.ds(1 + g * GROUP, GROUP), pl.ds((1 + g) * GROUP, GROUP)
        device = dev(m, r + (-1 if i == 0 else 1))
        return halo_pair(((1 + i, where), (1 + i, slice(None), wide)), ((to, where), (to, slice(None), wide)), ROWS * g + i, device)

    def side_halo(g):
        col, to, a = (1, COLS + 1, -1) if g == 0 else (COLS, 0, 1)
        wide, there = pl.ds((1 + g) * GROUP, GROUP), pl.ds((COLS + GROUP) * (1 - g), GROUP)
        copies = []
        for rows, to_rows, b in ((pl.ds(1, 2), pl.ds(1, 2), 0), (1, 3, -1), (2, 0, 1)):
            copies += halo_pair(
                ((rows, col), (rows, slice(None), wide)), ((to_rows, to), (to_rows, slice(None), there)), 4 + g, dev(m + a, r + b)
            )
        return copies

    def row_all(g, i):
        n = GROUP * K + 2 * GROUP
        return wait_for(n, ROWS * g + i)

    def side_all(g):
        return wait_for(4 * (K + 2 * GROUP), 4 + g)

    def wait_for(rows, sem):
        part = wts.at[pl.ds(0, rows), :]
        return remote(part, part, halo_send.at[sem], halo_recv.at[sem], (m, r))

    rest_of = places.at[:, pl.ds(0, BCOLS - COLS), :]
    place_all = remote(rest_of, rest_of, place_send.at[0], place_recv.at[0], (m, r))
    place_all.wait_recv()
    for g in range(2):
        gather_group(mine, places, seen_out, m, g)
        for d in range(1, NM):
            seen_copy(g, d).start()
        seen[g, pl.ds(m * MINE, MINE)] = seen_out[g, m]
    send_in(1)

    def arrive(g):
        seen_all(g).wait_recv()
        stack_group(seen, obs, stack, extra, g)
        for copy in row_halo(g, 0) + row_halo(g, 1) + side_halo(g):
            copy.start()

    def add(blocks):
        gram_blocks(stack, extra, ((lhs0, loc0), (lhs1, loc1)), gram, blocks, m, r)

    def own(g):
        return [(1 + i, 1 + g * GROUP + c) for i in range(ROWS) for c in range(GROUP)]

    def beyond(g):
        return [(3 * i, 1 + g * GROUP + c) for i in range(ROWS) for c in range(GROUP)]

    arrive(0)
    add(own(0))
    arrive(1)
    send_in(2)
    send_in(3)
    add(own(1))
    for i in range(ROWS):
        row_all(0, i).wait_recv()
    add(beyond(0))
    side_all(0).wait_recv()
    for i in range(ROWS):
        row_all(1, i).wait_recv()
    side_all(1).wait_recv()
    add(beyond(1) + [(tr, c) for tr in range(4) for c in (0, COLS + 1)])
    newton_schulz(gram, wts, y, z, mm, tmp, rest)

    def out_copy(q, d):
        g, i = q // ROWS, q % ROWS
        other = lax.rem(m + d, NM)
        src = result.at[pl.ds(other * MINE, MINE), i, pl.ds(pl.multiple_of(g * GROUP, GROUP), GROUP), :]
        dst = out.at[:, i, pl.ds(pl.multiple_of(m * COLS + g * GROUP, GROUP), GROUP), :]
        return remote(src, dst, out_send.at[q], out_recv.at[q], (other, r))

    def out_all(q):
        g, i = q // ROWS, q % ROWS
        part = result.at[pl.ds(0, K - MINE), i, pl.ds(pl.multiple_of(g * GROUP, GROUP), GROUP), :]
        return remote(part, part, out_send.at[q], out_recv.at[q], (m, r))

    def keep_copy(q):
        g, i = q // ROWS, q % ROWS
        src = result.at[pl.ds(m * MINE, MINE), i, pl.ds(pl.multiple_of(g * GROUP, GROUP), GROUP), :]
        dst = out.at[:, i, pl.ds(pl.multiple_of(m * COLS + g * GROUP, GROUP), GROUP), :]
        return pltpu.make_async_copy(src, dst, own_out.at[q])

    def chunk_out(q, carry):
        own_copy(q).wait()
        in_all(q).wait_recv()
        center_chunk(x, means, q // ROWS, q % ROWS)
        for pair in ((2, 6), (3, 5), (4, 1), (7, 0)):
            update_members(x, means, wts, result, q // ROWS, q % ROWS, [lax.rem(m + d, NM) for d in pair])
            for d in pair:
                (out_copy(q, d) if d else keep_copy(q)).start()
        return carry

    lax.fori_loop(0, len(CHUNKS), chunk_out, 0)

    obs_all.wait_send()
    place_all.wait_send()
    for g in range(2):
        seen_all(g).wait_send()
        side_all(g).wait_send()
        for i in range(ROWS):
            row_all(g, i).wait_send()
    for q in range(len(CHUNKS)):
        in_all(q).wait_send()
    for q in range(len(CHUNKS)):
        keep_copy(q).wait()
        out_all(q).wait_send()
        out_all(q).wait_recv()


def local(ensemble, obs_value, obs_error, obs_index, obs_count):
    dma = pltpu.SemaphoreType.DMA
    n = len(CHUNKS)
    square = pltpu.VMEM((K * K, 128), F32)
    hbm = [pltpu.with_memory_space_constraint(v, pltpu.MemorySpace.HBM) for v in (ensemble, obs_value, obs_error, obs_index, obs_count.reshape(1, BROWS))]
    return pl.pallas_call(
        kernel,
        out_shape=jax.ShapeDtypeStruct(ensemble.shape, F32),
        in_specs=[pl.BlockSpec(memory_space=pltpu.MemorySpace.HBM)] * 5,
        out_specs=pl.BlockSpec(memory_space=pl.ANY),
        scratch_shapes=[
            pltpu.SMEM((1, BROWS), jnp.int32),
            pltpu.VMEM((BROWS, 1, OBS), F32), pltpu.VMEM((BROWS, 1, OBS), F32), pltpu.VMEM((BROWS, 1, OBS), jnp.int32), dma((5,)),
            pltpu.VMEM((K, ROWS, COLS, VALS), F32),
            pltpu.VMEM((COLS, 4 * ROWS, OBS), F32),
            pltpu.VMEM((NR, 4 * ROWS, OBS), F32),
            pltpu.VMEM((ROWS + 2, COLS + 2, K, OBS), F32),
            pltpu.VMEM((ROWS + 2, 2, COLS + 2 * GROUP, OBS), F32),
            pltpu.VMEM((ROWS, COLS, VALS), F32),
            pltpu.VMEM((2 * PAIRS, DEEP * 128), BF16),
            pltpu.VMEM((256, DEEP * 128), BF16),
            pltpu.VMEM((2 * PAIRS, DEEP * 128), BF16),
            pltpu.VMEM((256, DEEP * 128), BF16),
            pltpu.VMEM((MINE, ROWS, BCOLS, VALS), F32),
            pltpu.VMEM((ROWS, BCOLS, OBS), F32),
            pltpu.VMEM((2, NM, MINE, ROWS, GROUP, OBS), F32),
            pltpu.VMEM((2, K, ROWS, GROUP, OBS), F32),
            pltpu.VMEM((PAIRS, 128), F32),
            square, square, square, square, square, square,
            pltpu.VMEM((K, ROWS, COLS, VALS), F32),
            dma((1,)), dma((1,)), dma((n,)), dma((n,)), dma((n,)),
            dma((6,)), dma((6,)), dma((n,)), dma((n,)), dma((n,)),
            dma((1,)), dma((1,)), dma((2,)), dma((2,)),
        ],
        compiler_params=pltpu.CompilerParams(collective_id=0, has_side_effects=True, vmem_limit_bytes=32 << 20),
    )(*hbm)


def solution(mesh):
    return jax.shard_map(
        local,
        mesh=mesh,
        in_specs=(
            P("member", "region", None, None),
            P(None, ("member", "region"), None),
            P(None, ("member", "region"), None),
            P(None, ("member", "region"), None),
            P(None, ("member", "region")),
        ),
        out_specs=P("member", "region", None, None),
        check_vma=False,
    )
```

time: 66.1 us -> 60.6 us (0.917)
  Pallas kernels: 63.1 us -> 59.2 us
  local copies, waits for them, and re-layouts: 2.76 us -> 1.15 us
    pallas_call x1, Pallas kernels: 63.1 us -> 59.2 us  [local(): pl.pallas_call(kernel, out_shape=jax.ShapeDtypeStruct(ensemble.shape, F32...]
    unnamed x1, local copies, waits for them, and re-layouts: 2.76 us -> 1.15 us
where the time goes in v3:
time: 60.6 us; the launch traced here: 60.4 us
  Pallas kernels  59.2 us (98%)
  local copies, waits for them, and re-layouts  1.15 us (2%)
    pallas_call x1, Pallas kernels, local(): pl.pallas_call(kernel, out_shape=jax.ShapeDtypeStruct(ensemble.shape, F32...  59.2 us

profile of v3, /device:TPU:1, one launch (start us, length us, event | category | flops | bytes accessed | tf_op | source)
XLA Modules:
  0.0 60.4 jit_solution(16429395433024658809)
XLA Ops:
  0.0 59.2 %shard_map.55 = f32[3,2,128,512]{3,2,1,0:T(8,128)S(1)} custom-call(f32[3,2,128,512]{3,2,1,0:T(8,128)} %ens.1, f32[32,1,128]{2,1,0:T(1,128)} %value_in.1, f32[32,1,128]{2,1,0:T(1,128)} %error_in.1, s32[32,1,128]{2,1,0:T(1,128)} %index_in.1, s32[1,32]{1,0:T(1,128)} %bitcast.1), custom_call_target="tpu_custom_call" | custom-call | tf_op jit(solution)/shard_map/pallas_call | solution.py:485
  59.2 1.1 %copy.7 = f32[3,2,128,512]{3,2,1,0:T(8,128)} copy(f32[3,2,128,512]{3,2,1,0:T(8,128)S(1)} %shard_map.55) | data formatting | bytes 3145728

commit v4 on v3

--- a/solution.py
+++ b/solution.py
@@ -193,13 +193,16 @@
             x[k, i, cols, lanes] = x[k, i, cols, lanes] - mean
 
 
+def rounded(v):
+    return v.astype(BF16).astype(F32)
+
+
 def gram_blocks(stack, extra, buffers, gram, blocks, m, r):
     sub = lax.broadcasted_iota(jnp.int32, (8, 128), 0)
     point_row = jnp.right_shift(sub, 2)
     center_row = (jnp.bitwise_and(jnp.right_shift(sub, 1), 1) * 8).astype(F32) + 3.5
     center_col = (jnp.bitwise_and(sub, 1) * 8).astype(F32) + 3.5
     zero = jnp.zeros((8, 128), F32)
-    blank = jnp.zeros((16, 128), BF16)
     for n, (tr, c) in enumerate(blocks):
         lhs, loc = buffers[n // DEEP % 2]
         lanes = pl.ds(n % DEEP * 128, 128)
@@ -218,30 +221,27 @@
                 dx = cell_col - center_col - float(SIDE * e)
                 weight = jnp.exp((dy * dy + dx * dx) * (-1.0 / (2.0 * LOC_SCALE * LOC_SCALE)))
                 reach[c - 1 + e] = jnp.where(keep, weight, 0.0)
-        for tile in range(COLS // 2):
-            if 2 * tile in reach or 2 * tile + 1 in reach:
-                both = jnp.concatenate([reach.get(2 * tile, zero), reach.get(2 * tile + 1, zero)], axis=0)
-                high = both.astype(BF16)
-                low = (both - high.astype(F32)).astype(BF16)
-            else:
-                high = low = blank
-            loc[pl.ds(16 * tile, 16), lanes] = high
-            loc[pl.ds(128 + 16 * tile, 16), lanes] = low
+        for col in range(COLS):
+            high = low = zero
+            if col in reach:
+                high = rounded(reach[col])
+                low = reach[col] - high
+            loc[pl.ds(8 * col, 8), lanes] = high
+            loc[pl.ds(128 + 8 * col, 8), lanes] = low
         members = [stack[tr, c, pl.ds(8 * gj, 8), :] for gj in range(3)]
         turned = [[pltpu.roll(v, 8 - d, 0) if d else v for d in range(8)] for v in members]
         innovation = jnp.broadcast_to(extra[tr, 0, pl.ds(AT + c, 1), :], (8, 128))
         pieces = [members[ga] * turned[gb][d] for ga, gb, d in TERMS] + [innovation * v for v in members]
         for t in range(PAIRS // 16):
             both = jnp.concatenate(pieces[2 * t : 2 * t + 2], axis=0)
-            high = both.astype(BF16)
-            lhs[pl.ds(16 * t, 16), lanes] = high
-            lhs[pl.ds(PAIRS + 16 * t, 16), lanes] = (both - high.astype(F32)).astype(BF16)
+            lhs[pl.ds(16 * t, 16), lanes] = both
+            lhs[pl.ds(PAIRS + 16 * t, 16), lanes] = both - rounded(both)
         if n % DEEP == DEEP - 1 or n == len(blocks) - 1:
             depth = pl.ds(0, 128 * (n % DEEP + 1))
             dims = (((1,), (1,)), ((), ()))
-            high = lax.dot_general(lhs[pl.ds(0, PAIRS), depth], loc[:, depth], dims, preferred_element_type=F32)
+            high = lax.dot_general(lhs[pl.ds(0, PAIRS), depth], loc[:, depth], dims, precision=lax.Precision.DEFAULT, preferred_element_type=F32)
             low = lax.dot_general(
-                lhs[pl.ds(PAIRS, PAIRS), depth], loc[pl.ds(0, 128), depth], dims, preferred_element_type=F32
+                lhs[pl.ds(PAIRS, PAIRS), depth], loc[pl.ds(0, 128), depth], dims, precision=lax.Precision.DEFAULT, preferred_element_type=F32
             )
             gram[...] = gram[...] + ((low + high[:, 128:]) + high[:, :128])
 
@@ -280,13 +280,13 @@
         pltpu.make_async_copy(src, dst, load.at[n])
         for n, (src, dst) in enumerate(((value_in, value), (error_in, error), (index_in, index), (count_in, count), (ens, mine)))
     ]
-    for copy in loads:
-        copy.start()
     barrier = pltpu.get_barrier_semaphore()
     around = [dev(m + d, r) for d in range(1, NM)] + [dev(m, r + d) for d in range(1, NR)]
     around += [dev(m + a, r + b) for a in (-1, 1) for b in (-1, 1)]
     for device in around:
         pl.semaphore_signal(barrier, inc=1, device_id=device, device_id_type=MESH)
+    for copy in loads:
+        copy.start()
     for copy in loads[:4]:
         copy.wait()
     sub = lax.broadcasted_iota(jnp.int32, (8, OBS), 0)
@@ -334,7 +334,7 @@
             (in_copy(q, d) if d else own_copy(q)).start()
 
     loads[4].wait()
-    send_in(0, (2, 6, 1, 7))
+    send_in(0)
     obs[r] = packed[r]
     gram[...] = jnp.zeros_like(gram)
     obs_all = remote(packed.at[pl.ds(0, NR - 1)], obs.at[pl.ds(0, NR - 1)], obs_send.at[0], obs_recv.at[0], (m, r))
@@ -359,7 +359,7 @@
             places[i, cols, :] = obs[pl.ds(g * GROUP, GROUP), i * 4 + 2, :]
     for d in range(1, NM):
         place_copy(d).start()
-    send_in(0, (3, 5, 4, 0))
+    send_in(1, (2, 6, 1, 7, 3, 5, 0))
 
     def halo_pair(src, dst, sem, device):
         return [remote(ref.at[a], ref.at[b], halo_send.at[sem], halo_recv.at[sem], device) for ref, a, b in zip((stack, extra), src, dst)]
@@ -399,12 +399,11 @@
         for d in range(1, NM):
             seen_copy(g, d).start()
         seen[g, pl.ds(m * MINE, MINE)] = seen_out[g, m]
-    send_in(1)
 
     def arrive(g):
         seen_all(g).wait_recv()
         stack_group(seen, obs, stack, extra, g)
-        for copy in row_halo(g, 0) + row_halo(g, 1) + side_halo(g):
+        for copy in side_halo(g) + row_halo(g, 0) + row_halo(g, 1):
             copy.start()
 
     def add(blocks):
@@ -417,19 +416,22 @@
         return [(3 * i, 1 + g * GROUP + c) for i in range(ROWS) for c in range(GROUP)]
 
     arrive(0)
+    send_in(1, (4,))
+    send_in(2, (2, 6, 1, 7))
     add(own(0))
     arrive(1)
-    send_in(2)
+    send_in(2, (3, 5, 4, 0))
     send_in(3)
     add(own(1))
     for i in range(ROWS):
         row_all(0, i).wait_recv()
     add(beyond(0))
     side_all(0).wait_recv()
+    add([(tr, COLS + 1) for tr in range(4)])
     for i in range(ROWS):
         row_all(1, i).wait_recv()
     side_all(1).wait_recv()
-    add(beyond(1) + [(tr, c) for tr in range(4) for c in (0, COLS + 1)])
+    add(beyond(1) + [(tr, 0) for tr in range(4)])
     newton_schulz(gram, wts, y, z, mm, tmp, rest)
 
     def out_copy(q, d):
@@ -496,10 +498,10 @@
             pltpu.VMEM((ROWS + 2, COLS + 2, K, OBS), F32),
             pltpu.VMEM((ROWS + 2, 2, COLS + 2 * GROUP, OBS), F32),
             pltpu.VMEM((ROWS, COLS, VALS), F32),
-            pltpu.VMEM((2 * PAIRS, DEEP * 128), BF16),
-            pltpu.VMEM((256, DEEP * 128), BF16),
-            pltpu.VMEM((2 * PAIRS, DEEP * 128), BF16),
-            pltpu.VMEM((256, DEEP * 128), BF16),
+            pltpu.VMEM((2 * PAIRS, DEEP * 128), F32),
+            pltpu.VMEM((256, DEEP * 128), F32),
+            pltpu.VMEM((2 * PAIRS, DEEP * 128), F32),
+            pltpu.VMEM((256, DEEP * 128), F32),
             pltpu.VMEM((MINE, ROWS, BCOLS, VALS), F32),
             pltpu.VMEM((ROWS, BCOLS, OBS), F32),
             pltpu.VMEM((2, NM, MINE, ROWS, GROUP, OBS), F32),
@@ -511,7 +513,7 @@
             dma((6,)), dma((6,)), dma((n,)), dma((n,)), dma((n,)),
             dma((1,)), dma((1,)), dma((2,)), dma((2,)),
         ],
-        compiler_params=pltpu.CompilerParams(collective_id=0, has_side_effects=True, vmem_limit_bytes=32 << 20),
+        compiler_params=pltpu.CompilerParams(collective_id=0, has_side_effects=True, vmem_limit_bytes=40 << 20),
     )(*hbm)
 
 

time: 60.6 us -> 58.7 us (0.969)
  Pallas kernels: 59.2 us -> 57.4 us
    pallas_call x1, Pallas kernels: 59.2 us -> 57.4 us  [local(): pl.pallas_call(kernel, out_shape=jax.ShapeDtypeStruct(ensemble.shape, F32...]
where the time goes in v4:
time: 58.7 us; the launch traced here: 58.5 us
  Pallas kernels  57.4 us (98%)
  local copies, waits for them, and re-layouts  1.15 us (2%)
    pallas_call x1, Pallas kernels, local(): pl.pallas_call(kernel, out_shape=jax.ShapeDtypeStruct(ensemble.shape, F32...  57.4 us

profile of v4, /device:TPU:1, one launch (start us, length us, event | category | flops | bytes accessed | tf_op | source)
XLA Modules:
  0.0 58.5 jit_solution(11921353282674147119)
XLA Ops:
  0.0 57.4 %shard_map.55 = f32[3,2,128,512]{3,2,1,0:T(8,128)S(1)} custom-call(f32[3,2,128,512]{3,2,1,0:T(8,128)} %ens.1, f32[32,1,128]{2,1,0:T(1,128)} %value_in.1, f32[32,1,128]{2,1,0:T(1,128)} %error_in.1, s32[32,1,128]{2,1,0:T(1,128)} %index_in.1, s32[1,32]{1,0:T(1,128)} %bitcast.1), custom_call_target="tpu_custom_call" | custom-call | tf_op jit(solution)/shard_map/pallas_call | solution.py:487
  57.4 1.1 %copy.7 = f32[3,2,128,512]{3,2,1,0:T(8,128)} copy(f32[3,2,128,512]{3,2,1,0:T(8,128)S(1)} %shard_map.55) | data formatting | bytes 3145728

commit v5 on v4

--- a/solution.py
+++ b/solution.py
@@ -162,6 +162,28 @@
                 ]
                 low, high = jnp.where(tile < 1, v[0], v[1]), jnp.where(tile < 3, v[2], v[3])
                 seen_out[g, other, u, i] = jnp.where(tile < 2, low, high)
+
+
+def stack_chunk(x, obs, stack, extra, means, i):
+    cols = pl.ds(0, GROUP)
+    center_chunk(x, means, 0, i)
+    root_weight = obs[cols, i * 4 + 0, :]
+    index = obs[cols, i * 4 + 2, :].astype(jnp.int32)
+    lane = jnp.bitwise_and(index, 127)
+    tile = jnp.right_shift(index, 7)
+
+    def pick(ref):
+        v = [
+            jnp.take_along_axis(ref[i, cols, pl.ds(128 * t, 128)], lane, axis=1, mode="promise_in_bounds")
+            for t in range(4)
+        ]
+        low, high = jnp.where(tile < 1, v[0], v[1]), jnp.where(tile < 3, v[2], v[3])
+        return jnp.where(tile < 2, low, high)
+
+    for k in range(K):
+        stack[1 + i, pl.ds(1, GROUP), k, :] = root_weight * pick(x.at[k])
+    extra[1 + i, 0, pl.ds(GROUP, GROUP), :] = root_weight * (obs[cols, i * 4 + 1, :] - pick(means))
+    extra[1 + i, 1, pl.ds(GROUP, GROUP), :] = jnp.bitwise_and(index, SIDE * SIDE - 1).astype(F32)
 
 
 def stack_group(seen, obs, stack, extra, g):
@@ -341,7 +363,7 @@
     obs_all.wait_recv()
 
     def place_copy(d):
-        own = places.at[:, pl.ds(pl.multiple_of(m * COLS, COLS), COLS), :]
+        own = places.at[:, pl.ds(pl.multiple_of(m * COLS + GROUP, GROUP), GROUP), :]
         return remote(own, own, place_send.at[0], place_recv.at[0], (lax.rem(m + d, NM), r))
 
     def seen_copy(g, d):
@@ -354,12 +376,11 @@
         return remote(part, part, seen_send.at[g], seen_recv.at[g], (m, r))
 
     for i in range(ROWS):
-        for g in range(2):
-            cols = pl.ds(pl.multiple_of(m * COLS + g * GROUP, GROUP), GROUP)
-            places[i, cols, :] = obs[pl.ds(g * GROUP, GROUP), i * 4 + 2, :]
+        cols = pl.ds(pl.multiple_of(m * COLS + GROUP, GROUP), GROUP)
+        places[i, cols, :] = obs[pl.ds(GROUP, GROUP), i * 4 + 2, :]
     for d in range(1, NM):
         place_copy(d).start()
-    send_in(1, (2, 6, 1, 7, 3, 5, 0))
+    send_in(1)
 
     def halo_pair(src, dst, sem, device):
         return [remote(ref.at[a], ref.at[b], halo_send.at[sem], halo_recv.at[sem], device) for ref, a, b in zip((stack, extra), src, dst)]
@@ -391,20 +412,21 @@
         part = wts.at[pl.ds(0, rows), :]
         return remote(part, part, halo_send.at[sem], halo_recv.at[sem], (m, r))
 
-    rest_of = places.at[:, pl.ds(0, BCOLS - COLS), :]
+    def arrive(i):
+        own_copy(i).wait()
+        in_all(i).wait_recv()
+        stack_chunk(x, obs, stack, extra, means, i)
+
+    arrive(0)
+    for copy in row_halo(0, 0):
+        copy.start()
+    rest_of = places.at[:, pl.ds(0, (NM - 1) * GROUP), :]
     place_all = remote(rest_of, rest_of, place_send.at[0], place_recv.at[0], (m, r))
     place_all.wait_recv()
-    for g in range(2):
-        gather_group(mine, places, seen_out, m, g)
-        for d in range(1, NM):
-            seen_copy(g, d).start()
-        seen[g, pl.ds(m * MINE, MINE)] = seen_out[g, m]
-
-    def arrive(g):
-        seen_all(g).wait_recv()
-        stack_group(seen, obs, stack, extra, g)
-        for copy in side_halo(g) + row_halo(g, 0) + row_halo(g, 1):
-            copy.start()
+    gather_group(mine, places, seen_out, m, 1)
+    for d in range(1, NM):
+        seen_copy(1, d).start()
+    seen[1, pl.ds(m * MINE, MINE)] = seen_out[1, m]
 
     def add(blocks):
         gram_blocks(stack, extra, ((lhs0, loc0), (lhs1, loc1)), gram, blocks, m, r)
@@ -415,11 +437,15 @@
     def beyond(g):
         return [(3 * i, 1 + g * GROUP + c) for i in range(ROWS) for c in range(GROUP)]
 
-    arrive(0)
-    send_in(1, (4,))
+    arrive(1)
+    for copy in side_halo(0) + row_halo(0, 1):
+        copy.start()
     send_in(2, (2, 6, 1, 7))
     add(own(0))
-    arrive(1)
+    seen_all(1).wait_recv()
+    stack_group(seen, obs, stack, extra, 1)
+    for copy in side_halo(1) + row_halo(1, 0) + row_halo(1, 1):
+        copy.start()
     send_in(2, (3, 5, 4, 0))
     send_in(3)
     add(own(1))
@@ -453,9 +479,12 @@
         return pltpu.make_async_copy(src, dst, own_out.at[q])
 
     def chunk_out(q, carry):
-        own_copy(q).wait()
-        in_all(q).wait_recv()
-        center_chunk(x, means, q // ROWS, q % ROWS)
+        @pl.when(q >= ROWS)
+        def _():
+            own_copy(q).wait()
+            in_all(q).wait_recv()
+            center_chunk(x, means, q // ROWS, q % ROWS)
+
         for pair in ((2, 6), (3, 5), (4, 1), (7, 0)):
             update_members(x, means, wts, result, q // ROWS, q % ROWS, [lax.rem(m + d, NM) for d in pair])
             for d in pair:
@@ -466,8 +495,8 @@
 
     obs_all.wait_send()
     place_all.wait_send()
+    seen_all(1).wait_send()
     for g in range(2):
-        seen_all(g).wait_send()
         side_all(g).wait_send()
         for i in range(ROWS):
             row_all(g, i).wait_send()

time: 58.7 us -> 55.2 us (0.940)
  Pallas kernels: 57.4 us -> 53.7 us
    pallas_call x1, Pallas kernels: 57.4 us -> 53.7 us  [local(): pl.pallas_call(kernel, out_shape=jax.ShapeDtypeStruct(ensemble.shape, F32...]
where the time goes in v5:
time: 55.2 us; the launch traced here: 54.9 us
  Pallas kernels  53.7 us (97%)
  local copies, waits for them, and re-layouts  1.15 us (2%)
    pallas_call x1, Pallas kernels, local(): pl.pallas_call(kernel, out_shape=jax.ShapeDtypeStruct(ensemble.shape, F32...  53.7 us
    unnamed x1, local copies, waits for them, and re-layouts  1.15 us

profile of v5, /device:TPU:1, one launch (start us, length us, event | category | flops | bytes accessed | tf_op | source)
XLA Modules:
  0.0 54.9 jit_solution(8525535200058361502)
XLA Ops:
  0.0 53.7 %shard_map.55 = f32[3,2,128,512]{3,2,1,0:T(8,128)S(1)} custom-call(f32[3,2,128,512]{3,2,1,0:T(8,128)} %ens.1, f32[32,1,128]{2,1,0:T(1,128)} %value_in.1, f32[32,1,128]{2,1,0:T(1,128)} %error_in.1, s32[32,1,128]{2,1,0:T(1,128)} %index_in.1, s32[1,32]{1,0:T(1,128)} %bitcast.1), custom_call_target="tpu_custom_call" | custom-call | tf_op jit(solution)/shard_map/pallas_call | solution.py:516
  53.8 1.1 %copy.7 = f32[3,2,128,512]{3,2,1,0:T(8,128)} copy(f32[3,2,128,512]{3,2,1,0:T(8,128)S(1)} %shard_map.55) | data formatting | bytes 3145728

commit v6 on v5

--- a/solution.py
+++ b/solution.py
@@ -485,7 +485,7 @@
             in_all(q).wait_recv()
             center_chunk(x, means, q // ROWS, q % ROWS)
 
-        for pair in ((2, 6), (3, 5), (4, 1), (7, 0)):
+        for pair in ((2,), (6,), (3, 5), (4, 1), (7, 0)):
             update_members(x, means, wts, result, q // ROWS, q % ROWS, [lax.rem(m + d, NM) for d in pair])
             for d in pair:
                 (out_copy(q, d) if d else keep_copy(q)).start()

time: 55.2 us -> 55.2 us (level)
  no operation moved by 1% of the time
where the time goes in v6:
time: 55.2 us; the launch traced here: 54.8 us
  Pallas kernels  53.7 us (97%)
  local copies, waits for them, and re-layouts  1.15 us (2%)
    pallas_call x1, Pallas kernels, local(): pl.pallas_call(kernel, out_shape=jax.ShapeDtypeStruct(ensemble.shape, F32...  53.7 us
    unnamed x1, local copies, waits for them, and re-layouts  1.15 us

profile of v6, /device:TPU:1, one launch (start us, length us, event | category | flops | bytes accessed | tf_op | source)
XLA Modules:
  0.0 54.8 jit_solution(7871566712467938889)
XLA Ops:
  0.0 53.7 %shard_map.55 = f32[3,2,128,512]{3,2,1,0:T(8,128)S(1)} custom-call(f32[3,2,128,512]{3,2,1,0:T(8,128)} %ens.1, f32[32,1,128]{2,1,0:T(1,128)} %value_in.1, f32[32,1,128]{2,1,0:T(1,128)} %error_in.1, s32[32,1,128]{2,1,0:T(1,128)} %index_in.1, s32[1,32]{1,0:T(1,128)} %bitcast.1), custom_call_target="tpu_custom_call" | custom-call | tf_op jit(solution)/shard_map/pallas_call | solution.py:516
  53.7 1.1 %copy.7 = f32[3,2,128,512]{3,2,1,0:T(8,128)} copy(f32[3,2,128,512]{3,2,1,0:T(8,128)S(1)} %shard_map.55) | data formatting | bytes 3145728
